TPU v7x, 16 devices: a whole 2x2x2 slice. The times are simulated.
16 devices in a mesh: sp: 16 (over z, y, x, core).
Axes of the slice: x: 2, y: 2, z: 2, core: 2. Of those that a mesh axis runs over, the one named last changes fastest.
Arguments:
- x: bfloat16 [4, 2048, 2560], P(None, 'sp')
- ln1_w: bfloat16 [2560], replicated
- w_qkv: bfloat16 [2560, 7680], replicated
- q_ln_w: bfloat16 [32, 80], replicated
- k_ln_w: bfloat16 [32, 80], replicated
- w_out: bfloat16 [2560, 2560], replicated
- grad_y: bfloat16 [4, 2048, 2560], P(None, 'sp')
Outputs:
- output 1: bfloat16 [4, 2048, 2560], P(None, 'sp')
- output 2: bfloat16 [4, 2048, 2560], P(None, 'sp')
- output 3: float32 [2560], replicated
- output 4: float32 [2560, 7680], replicated
- output 5: float32 [32, 80], replicated
- output 6: float32 [32, 80], replicated
- output 7: float32 [2560, 2560], replicated
All inputs are finite; a program needn't handle non-finite values.
Results may differ from a plain program's by a relative error of at most 0.0121307.
Values are sent between devices in bfloat16 or wider.
A program may use at most 1 GiB of HBM per device.

v0:
```python
import math
import jax
import jax.numpy as jnp
from jax import lax
from jax.sharding import PartitionSpec as P


def alibi_slopes(n_heads):
    pow_two = 2 ** math.ceil(math.log2(n_heads))
    exponents = jnp.arange(1, pow_two + 1, dtype=jnp.float32) * (8.0 / pow_two)
    slopes = jnp.exp2(-exponents)
    if pow_two != n_heads:
        slopes = jnp.concatenate([slopes[1::2], slopes[0::2]])[:n_heads]
    return slopes


def layer_norm(values, weight):
    centered = values - jnp.mean(values, axis=-1, keepdims=True)
    var_val = jnp.mean(centered * centered, axis=-1, keepdims=True)
    return centered * lax.rsqrt(var_val + 1e-5) * weight


def block_scores(q_cur, k_all, slopes, q_start, score_scale):
    q_count = q_cur.shape[1]
    k_count = k_all.shape[1]
    scores = jnp.einsum('bqhd,bkhd->bhqk', q_cur, k_all, preferred_element_type=jnp.float32) * score_scale
    pos_gap = (q_start + jnp.arange(q_count))[:, None] - jnp.arange(k_count)[None, :]
    biased = scores - slopes[:, None, None] * pos_gap.astype(jnp.float32)
    return jnp.where(pos_gap >= 0, biased, -1e30)


def attn_forward(q_loc, k_all, v_all, slopes, q_offset, q_blk):
    n_batch, q_len, n_heads, head_dim = q_loc.shape
    n_blk = q_len // q_blk
    score_scale = head_dim ** -0.5
    q_blocks = q_loc.reshape(n_batch, n_blk, q_blk, n_heads, head_dim)

    def one_block(blk_idx):
        q_cur = lax.dynamic_index_in_dim(q_blocks, blk_idx, axis=1, keepdims=False)
        scores = block_scores(q_cur, k_all, slopes, q_offset + blk_idx * q_blk, score_scale)
        row_max = jnp.max(scores, axis=-1)
        weights = jnp.exp(scores - row_max[..., None])
        row_sum = jnp.sum(weights, axis=-1)
        weighted = jnp.einsum('bhqk,bkhd->bqhd', weights.astype(jnp.bfloat16), v_all, preferred_element_type=jnp.float32)
        out_blk = weighted / jnp.swapaxes(row_sum, 1, 2)[..., None]
        return out_blk.astype(jnp.bfloat16), row_max + jnp.log(row_sum)

    out_blocks, lse_blocks = lax.map(one_block, jnp.arange(n_blk))
    out_all = jnp.moveaxis(out_blocks, 0, 1).reshape(n_batch, q_len, n_heads, head_dim)
    return out_all, lse_blocks


def attn_backward(q_loc, k_all, v_all, out_all, d_out, lse_blocks, slopes, q_offset, q_blk):
    n_batch, q_len, n_heads, head_dim = q_loc.shape
    n_blk = q_len // q_blk
    score_scale = head_dim ** -0.5
    q_blocks = q_loc.reshape(n_batch, n_blk, q_blk, n_heads, head_dim)
    do_blocks = d_out.reshape(n_batch, n_blk, q_blk, n_heads, head_dim)
    row_dot = jnp.einsum('bqhd,bqhd->bhq', d_out, out_all, preferred_element_type=jnp.float32).reshape(n_batch, n_heads, n_blk, q_blk)

    def one_block(acc_pair, blk_idx):
        dk_acc, dv_acc = acc_pair
        q_cur = lax.dynamic_index_in_dim(q_blocks, blk_idx, axis=1, keepdims=False)
        do_cur = lax.dynamic_index_in_dim(do_blocks, blk_idx, axis=1, keepdims=False)
        delta_cur = lax.dynamic_index_in_dim(row_dot, blk_idx, axis=2, keepdims=False)
        lse_cur = lax.dynamic_index_in_dim(lse_blocks, blk_idx, axis=0, keepdims=False)
        scores = block_scores(q_cur, k_all, slopes, q_offset + blk_idx * q_blk, score_scale)
        prob_blk = jnp.exp(scores - lse_cur[..., None])
        dv_acc = dv_acc + jnp.einsum('bhqk,bqhd->bkhd', prob_blk.astype(jnp.bfloat16), do_cur, preferred_element_type=jnp.float32)
        d_probs = jnp.einsum('bqhd,bkhd->bhqk', do_cur, v_all, preferred_element_type=jnp.float32)
        d_scores = (prob_blk * (d_probs - delta_cur[..., None]) * score_scale).astype(jnp.bfloat16)
        dq_cur = jnp.einsum('bhqk,bkhd->bqhd', d_scores, k_all, preferred_element_type=jnp.float32)
        dk_acc = dk_acc + jnp.einsum('bhqk,bqhd->bkhd', d_scores, q_cur, preferred_element_type=jnp.float32)
        return (dk_acc, dv_acc), dq_cur.astype(jnp.bfloat16)

    zero_acc = jnp.zeros(k_all.shape, jnp.float32)
    acc_final, dq_blocks = lax.scan(one_block, (zero_acc, zero_acc), jnp.arange(n_blk))
    d_q = jnp.moveaxis(dq_blocks, 0, 1).reshape(n_batch, q_len, n_heads, head_dim)
    return d_q, acc_final[0], acc_final[1]


def solution(mesh):
    n_sp = mesh.shape['sp']
    seq_spec = P(None, 'sp', None)
    rep_spec = P()

    def local_step(x, ln1_w, w_qkv, q_ln_w, k_ln_w, w_out, grad_y):
        n_batch, tok_loc, d_model = x.shape
        n_heads, head_dim = q_ln_w.shape
        heads_loc = n_heads // n_sp
        seq_len = tok_loc * n_sp
        head_base = lax.axis_index('sp') * heads_loc
        slopes = lax.dynamic_slice_in_dim(alibi_slopes(n_heads), head_base, heads_loc)
        head_shape = (n_batch, tok_loc, n_heads, head_dim)
        flat_shape = (n_batch, tok_loc, d_model)
        x_f32 = x.astype(jnp.float32)
        h_f32, ln1_pull = jax.vjp(layer_norm, x_f32, ln1_w.astype(jnp.float32))
        h_act = h_f32.astype(jnp.bfloat16)
        qkv_raw = jnp.einsum('btd,de->bte', h_act, w_qkv, preferred_element_type=jnp.float32)
        q_f32, q_pull = jax.vjp(layer_norm, qkv_raw[..., :d_model], q_ln_w.reshape(d_model).astype(jnp.float32))
        k_f32, k_pull = jax.vjp(layer_norm, qkv_raw[..., d_model:2 * d_model], k_ln_w.reshape(d_model).astype(jnp.float32))
        qkv_tok = jnp.stack([q_f32.astype(jnp.bfloat16).reshape(head_shape), k_f32.astype(jnp.bfloat16).reshape(head_shape), qkv_raw[..., 2 * d_model:].astype(jnp.bfloat16).reshape(head_shape)])
        qkv_head = lax.all_to_all(qkv_tok, 'sp', 3, 2, tiled=True)
        q_blk = math.gcd(seq_len, 256)
        o_head, lse_blocks = attn_forward(qkv_head[0], qkv_head[1], qkv_head[2], slopes, 0, q_blk)
        o_tok = lax.all_to_all(o_head, 'sp', 1, 2, tiled=True).reshape(flat_shape)
        y = (jnp.einsum('btd,de->bte', o_tok, w_out, preferred_element_type=jnp.float32) + x_f32).astype(jnp.bfloat16)
        grad_w_out = jnp.einsum('btd,bte->de', o_tok, grad_y, preferred_element_type=jnp.float32)
        d_o = jnp.einsum('bte,de->btd', grad_y, w_out, preferred_element_type=jnp.float32).astype(jnp.bfloat16)
        d_o_head = lax.all_to_all(d_o.reshape(head_shape), 'sp', 2, 1, tiled=True)
        d_q, d_k, d_v = attn_backward(qkv_head[0], qkv_head[1], qkv_head[2], o_head, d_o_head, lse_blocks, slopes, 0, q_blk)
        d_qkv_head = jnp.stack([d_q, d_k.astype(jnp.bfloat16), d_v.astype(jnp.bfloat16)])
        d_qkv_tok = lax.all_to_all(d_qkv_head, 'sp', 2, 3, tiled=True)
        dq_raw, grad_q_ln = q_pull(d_qkv_tok[0].reshape(flat_shape).astype(jnp.float32))
        dk_raw, grad_k_ln = k_pull(d_qkv_tok[1].reshape(flat_shape).astype(jnp.float32))
        d_qkv = jnp.concatenate([dq_raw.astype(jnp.bfloat16), dk_raw.astype(jnp.bfloat16), d_qkv_tok[2].reshape(flat_shape)], axis=-1)
        grad_w_qkv = jnp.einsum('btd,bte->de', h_act, d_qkv, preferred_element_type=jnp.float32)
        d_h = jnp.einsum('bte,de->btd', d_qkv, w_qkv, preferred_element_type=jnp.float32).astype(jnp.bfloat16)
        d_x_norm, grad_ln1 = ln1_pull(d_h.astype(jnp.float32))
        grad_x = (d_x_norm + grad_y.astype(jnp.float32)).astype(jnp.bfloat16)
        weight_grads = lax.psum((grad_ln1, grad_w_qkv, grad_q_ln.reshape(n_heads, head_dim), grad_k_ln.reshape(n_heads, head_dim), grad_w_out), 'sp')
        return (y, grad_x) + tuple(weight_grads)

    return jax.shard_map(local_step, mesh=mesh, in_specs=(seq_spec, rep_spec, rep_spec, rep_spec, rep_spec, rep_spec, seq_spec), out_specs=(seq_spec, seq_spec, rep_spec, rep_spec, rep_spec, rep_spec, rep_spec), check_vma=False)
```

profile of v0, /device:TPU:1, one launch (start us, length us, event | category | flops | bytes accessed | tf_op | source)
XLA Modules:
  0.0 2246.5 jit_solution(1219698249488174087)
XLA Ops:
  31.8 28.0 %fusion.56 = f32[4,128,7680]{2,1,0:T(8,128)} fusion(bf16[2560,7680]{1,0:T(8,128)(2,1)} %param.13, bf16[4,128,2560]{2,1,0:T(8,128)(2,1)S(1)} %copy-done.3, f32[2560]{0:T(1024)S(1)} %convert_element_type.111, f32[4,128]{1,0:T(4,128)S(1)} %fusion.87, f32[4,128]{1,0:T(4,128)S(1)} %broadcast_multiply_fusion.4), kind=kOutput, calls=%fused_computation.60 | convolution fusion | flops 20139212800 | bytes 57686016 | tf_op jit(solution)/shard_map/btd,de->bte/dot_general | solution.py:99
  115.7 86.9 %all-to-all-done = bf16[3,4,128,32,80]{2,4,1,0,3:T(8,128)(2,1)} async-done(((bf16[3,4,128,32,80]{2,4,1,0,3:T(8,128)(2,1)}), bf16[3,4,128,32,80]{2,4,1,0,3:T(8,128)(2,1)}, u32[]{:S(2)}, u32[]{:S(2)}) %all-to-all-start) | async-done | bytes 7864352 | tf_op jit(solution)/shard_map/all_to_all | solution.py:103
  234.0 259.2 %while.27 = (s32[]{:T(128)}, bf16[8,4,256,2,80]{2,4,3,1,0:T(8,128)(2,1)}, f32[8,4,2,256]{3,2,1,0:T(2,128)S(1)}, s32[8]{0:T(128)S(1)}, bf16[4,8,256,2,80]{2,4,3,0...) while((s32[]{:T(128)}, ...), condition=%wide.region_9.10_spmd, body=%wide.region_6.9_spmd.sunk | while | flops 1404369152 | bytes 89853160 | solution.py:48
  517.0 430.3 %while.28 = (s32[]{:T(128)}, f32[4,2048,2,80]{1,3,2,0:T(8,128)}, f32[4,2048,2,80]{1,3,2,0:T(8,128)}, bf16[8,4,256,2,80]{2,4,3,1,0:T(8,128)(2,1)}, s32[8]{0:T(128...) while((s32[]{:T(128)}, f32[4,2048,2,80]{1,3,2,0:T(8,128)}, ...), condition=%wide.region_11.12_spmd.clone, body=%wide.region_10.11_spmd.clone.sunk | while | flops 3418521856 | bytes 168439088 | solution.py:77
  542.8 13.2 multiply_convert_fusion.4
  595.2 13.2 multiply_convert_fusion.4
  649.2 13.2 multiply_convert_fusion.4
  703.2 13.2 multiply_convert_fusion.4
  757.3 13.2 multiply_convert_fusion.4
  811.3 13.2 multiply_convert_fusion.4
  865.4 13.2 multiply_convert_fusion.4
  907.5 11.9 bitcast_add_fusion.5
  919.4 13.2 multiply_convert_fusion.4
  965.9 30.7 %copy.82 = bf16[3,4,2048,2,80]{4,3,1,0,2:T(2,128)(2,1)} copy(bf16[3,4,2048,2,80]{2,4,3,1,0:T(8,128)(2,1)} %pad_maximum_fusion.1) | data formatting | bytes 15728640 | tf_op jit(solution)/shard_map/stack | solution.py:112
  1009.7 14.2 convolution_bitcast_fusion.1
  1023.8 132.7 %all-to-all-done.3 = bf16[3,4,2048,2,80]{4,3,1,0,2:T(2,128)(2,1)} async-done(((bf16[3,4,2048,2,80]{4,3,1,0,2:T(2,128)(2,1)}), bf16[3,4,2048,2,80]{4,3,1,0,2:T(2,128)(2,1)}, u32[]{:S(2)}, u32[]{:S(2)}) %all-to-all-start.3) | async-done | bytes 7864352 | tf_op jit(solution)/shard_map/all_to_all | solution.py:113
  1156.6 20.2 copy.104
  1238.1 34.2 %convolution_bitcast_fusion = f32[2560,7680]{1,0:T(8,128)} fusion(bf16[4,128,2560]{2,1,0:T(8,128)(2,1)} %copy.89, bf16[4,128,2560]{2,1,0:T(8,128)(2,1)} %get-tuple-element.277, bf16[4,128,2560]{2,1,0:T(8,128)(2,1)} %get-tuple-element.276, bf16[4,128,2560]{2,1,0:T(8,128)(2,1)S(1)} %copy-done.4, f32[2560]{0:T(1024)S(1)} %copy-done.10, ...), kind=kOutput, calls=%fused_computation.57 | convolution fusion | flops 20162805760 | bytes 89143296 | tf_op jit(solution)/shard_map/btd,bte->de/dot_general | solution.py:117
  1272.3 12.1 fusion.72
  1284.5 30.0 %fusion.71 = (f32[4,128]{1,0:T(4,128)S(1)}, bf16[4,128,2560]{2,1,0:T(8,128)(2,1)}) fusion(bf16[4,128,2560]{2,1,0:T(8,128)(2,1)S(1)} %copy-done.4, f32[2560]{0:T(1024)S(1)} %copy-done.10, f32[4,128]{1,0:T(4,128)S(1)} %copy-done.8, bf16[2560,7680]{1,0:T(8,128)(2,1)} %param.13, bf16[4,128,2560]{2,1,0:T(8,128)(2,1)} %copy.89, ...), kind=kOutput, calls=%fused_computation.88 | convolution fusion | flops 20165427200 | bytes 52443136 | tf_op jit(solution)/shard_map/bte,de->btd/dot_general | solution.py:118
  1318.3 34.8 %all-reduce = (f32[2560]{0:T(1024)}, f32[32,80]{1,0:T(8,128)}, f32[32,80]{1,0:T(8,128)}) all-reduce(f32[2560]{0:T(1024)S(1)} %get-tuple-element.227, f32[32,80]{1,0:T(8,128)S(1)} %reshape.232, f32[32,80]{1,0:T(8,128)S(1)} %reshape.233), channel_id=1, replica_groups=mesh['sp'=16] {'sp'}, use_global_device_ids=true, to_apply=%region_19.20 | all-reduce | flops 7680 | bytes 61440 | tf_op jit(solution)/shard_map/psum | solution.py:121
  1358.3 812.1 %all-reduce.4.cloned.1.call-done = (f32[2560,7680]{1,0:T(8,128)}, f32[2560,2560]{1,0:T(8,128)}) async-done(((f32[2560,7680]{1,0:T(8,128)}, f32[2560,2560]{1,0:T(8,128)}), (f32[2560,7680]{1,0:T(8,128)}, f32[2560,2560]{1,0:T(8,128)})) %all-reduce.4.cloned.1.call-update) | async-done | bytes 104857616 | tf_op jit(solution)/shard_map/psum | solution.py:121
  2170.3 51.5 %copy.141 = f32[2560,7680]{1,0:T(8,128)} copy(f32[2560,7680]{1,0:T(8,128)} %get-tuple-element.503) | data formatting | bytes 157286400
  2221.8 17.6 copy.142
  (376 shorter events, 766.0 us)
Async XLA Ops:
  20.5 9.4 copy-start.3
  24.3 73.8 %all-to-all-start.2 = ((bf16[4,128,32,80]{1,3,0,2:T(8,128)(2,1)}), bf16[4,128,32,80]{1,3,0,2:T(8,128)(2,1)}, u32[]{:S(2)}, u32[]{:S(2)}) async-start(bf16[4,128,32,80]{1,3,0,2:T(8,128)(2,1)} %copy.76), calls=%async_computation.2 | async-start | bytes 5242880 | tf_op jit(solution)/shard_map/all_to_all | solution.py:110
  30.3 29.5 %copy-start.7 = (f32[4,128]{1,0:T(4,128)}, f32[4,128]{1,0:T(4,128)S(1)}, u32[]{:S(2)}) copy-start(f32[4,128]{1,0:T(4,128)S(1)} %broadcast_multiply_fusion.4) | copy-start | bytes 6148
  31.8 28.1 %copy-start.11 = (f32[4,128]{1,0:T(4,128)}, f32[4,128]{1,0:T(4,128)S(1)}, u32[]{:S(2)}) copy-start(f32[4,128]{1,0:T(4,128)S(1)} %fusion.87) | copy-start | bytes 6148
  31.8 28.0 %copy-start.9 = (f32[2560]{0:T(1024)}, f32[2560]{0:T(1024)S(1)}, u32[]{:S(2)}) copy-start(f32[2560]{0:T(1024)S(1)} %convert_element_type.111) | copy-start | bytes 30724
  98.1 104.5 %all-to-all-start = ((bf16[3,4,128,32,80]{2,4,1,0,3:T(8,128)(2,1)}), bf16[3,4,128,32,80]{2,4,1,0,3:T(8,128)(2,1)}, u32[]{:S(2)}, u32[]{:S(2)}) async-start(bf16[3,4,128,32,80]{2,4,1,0,3:T(8,128)(2,1)} %copy.67), calls=%async_computation | async-start | bytes 15728640 | tf_op jit(solution)/shard_map/all_to_all | solution.py:103
  511.3 485.4 %all-to-all-start.1 = ((bf16[4,2048,2,80]{3,2,0,1:T(2,128)(2,1)}), bf16[4,2048,2,80]{3,2,0,1:T(2,128)(2,1)}, u32[]{:S(2)}, u32[]{:S(2)}) async-start(bf16[4,2048,2,80]{3,2,0,1:T(2,128)(2,1)} %copy.71), calls=%async_computation.1 | async-start | bytes 8388608 | tf_op jit(solution)/shard_map/all_to_all | solution.py:106
  952.0 8.4 slice-start.4
  996.7 159.9 %all-to-all-start.3 = ((bf16[3,4,2048,2,80]{4,3,1,0,2:T(2,128)(2,1)}), bf16[3,4,2048,2,80]{4,3,1,0,2:T(2,128)(2,1)}, u32[]{:S(2)}, u32[]{:S(2)}) async-start(bf16[3,4,2048,2,80]{4,3,1,0,2:T(2,128)(2,1)} %copy.82), calls=%async_computation.3 | async-start | bytes 25165824 | tf_op jit(solution)/shard_map/all_to_all | solution.py:113
  1000.5 1169.8 %all-reduce.4.cloned.1.call-start = ((), (), s32[]{:S(2)}) async-start(), calls=%async_computation.4 | async-start | bytes 209715200 | tf_op jit(solution)/shard_map/psum | solution.py:121
  1009.6 14.2 copy-start.6
  1206.6 11.1 copy-start.30
  1206.6 11.1 copy-start.14
  1206.6 11.1 copy-start.20
  1206.6 11.1 copy-start.24
  1212.6 14.4 slice-start
  1212.6 14.4 slice-start.1
  1212.6 14.4 slice-start.6
  1217.7 9.3 copy-start.28
  1217.7 10.1 slice-start.2
  1217.7 10.9 slice-start.3
  1217.7 11.1 slice-start.7
  1217.7 11.1 copy-start.22
  1284.5 30.0 %copy-start.26 = (f32[4,128]{1,0:T(4,128)S(1)}, f32[4,128]{1,0:T(4,128)}, u32[]{:S(2)}) copy-start(f32[4,128]{1,0:T(4,128)} %copy-done.25) | copy-start | bytes 6148
  (44 other events, 189.7 us)
Sparse Core Ops, SparseCore 0:
  1272.4 897.8 all-reduce.3
where the time goes:
time: 2250 us
  waiting for transfers between devices  1030 us (46%)
  matrix products  672 us (30%)
  local copies, waits for them, and re-layouts  276 us (12%)
  other arithmetic  157 us (7%)
  loops' own time  43.1 us (2%)
  blocking collectives  34.8 us (2%)
    psum x1, waiting for transfers between devices, local_step(): lax.psum((grad_ln1, grad_w_qkv, grad_q_ln.reshape(n_heads, head_dim), gra...  812 us
    dot_general x16, matrix products, block_scores(): jnp.einsum('bqhd,bkhd->bhqk', q_cur, k_all, preferred_element_type=jnp.fl...  151 us
    all_to_all x1, waiting for transfers between devices, local_step(): d_qkv_tok = lax.all_to_all(d_qkv_head, 'sp', 2, 3, tiled=True)  133 us
    dot_general x8, matrix products, one_block(): jnp.einsum('bqhd,bkhd->bhqk', do_cur, v_all, preferred_element_type=jnp.f...  106 us
    dot_general x8, matrix products, one_block(): jnp.einsum('bhqk,bqhd->bkhd', prob_blk.astype(jnp.bfloat16), do_cur, pref...  94 us
    all_to_all x1, waiting for transfers between devices, local_step(): qkv_head = lax.all_to_all(qkv_tok, 'sp', 3, 2, tiled=True)  86.9 us
    dot_general x8, matrix products, one_block(): jnp.einsum('bhqk,bkhd->bqhd', weights.astype(jnp.bfloat16), v_all, prefer...  77.4 us
    unnamed x81, local copies, waits for them, and re-layouts  77.4 us
  transfers between devices with their start and end apart: 5, of which 3 were waited for; matrix products, arithmetic and copies ran while one was open for 27% of the time, Pallas kernels for 0%

commit v1 on v0

v1 whole, which is shorter than its diff:
```python
import functools
import math
import jax
import jax.numpy as jnp
from jax import lax
from jax.experimental import pallas as pl
from jax.experimental.pallas import tpu as pltpu
from jax.sharding import PartitionSpec as P

F32 = jnp.float32
BF16 = jnp.bfloat16
LANES = 128
LOG2E = math.log2(math.e)
MESH = pl.DeviceIdType.MESH


def alibi_slopes(n_heads):
    pow_two = 2 ** math.ceil(math.log2(n_heads))
    exponents = jnp.arange(1, pow_two + 1, dtype=F32) * (8.0 / pow_two)
    slopes = jnp.exp2(-exponents)
    if pow_two != n_heads:
        slopes = jnp.concatenate([slopes[1::2], slopes[0::2]])[:n_heads]
    return slopes


def layer_norm(values, weight):
    centered = values - jnp.mean(values, axis=-1, keepdims=True)
    var_val = jnp.mean(centered * centered, axis=-1, keepdims=True)
    return centered * lax.rsqrt(var_val + 1e-5) * weight


def row_stats(values):
    mean = jnp.mean(values, axis=-1, keepdims=True)
    centered = values - mean
    var_val = jnp.mean(centered * centered, axis=-1)
    return mean[..., 0], lax.rsqrt(var_val + 1e-5)


def exchange(block, n_dev):
    def kernel(x_ref, o_ref, loc_sem, send_sem, recv_sem):
        me = lax.axis_index('sp')
        own = pltpu.make_async_copy(x_ref, o_ref.at[me], loc_sem)
        own.start()
        copies = []
        for step in range(1, n_dev):
            copies.append(pltpu.make_async_remote_copy(
                src_ref=x_ref, dst_ref=o_ref.at[me], send_sem=send_sem.at[step], recv_sem=recv_sem.at[step],
                device_id=(lax.rem(me + step, n_dev),), device_id_type=MESH))
            copies[-1].start()
        own.wait()
        for copy in copies:
            copy.wait()

    return pl.pallas_call(
        kernel,
        out_shape=jax.ShapeDtypeStruct((n_dev,) + block.shape, block.dtype),
        in_specs=[pl.BlockSpec(memory_space=pl.ANY)],
        out_specs=pl.BlockSpec(memory_space=pl.ANY),
        scratch_shapes=[pltpu.SemaphoreType.DMA, pltpu.SemaphoreType.DMA((n_dev,)), pltpu.SemaphoreType.DMA((n_dev,))],
        compiler_params=pltpu.CompilerParams(has_side_effects=True),
        name='exchange',
    )(block)


def qkv_heads(h_all, w_pad, stats, gains, n_dev, n_batch, tok, seq):
    rows = n_batch * tok
    d_model = h_all.shape[-1]
    n_h = gains.shape[0] // 2

    def kernel(h_ref, w_ref, st_ref, g_ref, q_ref, k_ref, v_ref, xq_ref, xk_ref):
        raw = jnp.dot(h_ref[...], w_ref[...], preferred_element_type=F32)
        st = st_ref[...]
        for n in range(n_h):
            for part, (o_ref, x_ref) in enumerate(((q_ref, xq_ref), (k_ref, xk_ref))):
                col = (part * n_h + n) * LANES
                hat = (raw[:, col:col + LANES] - st[:, 2 * part:2 * part + 1]) * st[:, 2 * part + 1:2 * part + 2]
                out = (hat * g_ref[part * n_h + n:part * n_h + n + 1, :]).astype(BF16)
                x_ref[:, n] = hat.reshape(n_batch, tok, LANES)
                o_ref[:, n] = out.reshape(n_batch, tok, LANES)
            col = (2 * n_h + n) * LANES
            v_ref[:, n] = raw[:, col:col + LANES].astype(BF16).reshape(n_batch, tok, LANES)

    shape = (n_batch, n_h, seq, LANES)
    spec = pl.BlockSpec((n_batch, n_h, tok, LANES), lambda i: (0, 0, i, 0))
    n_col = w_pad.shape[1]
    return pl.pallas_call(
        kernel,
        grid=(n_dev,),
        out_shape=[jax.ShapeDtypeStruct(shape, BF16)] * 3 + [jax.ShapeDtypeStruct(shape, F32)] * 2,
        in_specs=[pl.BlockSpec((rows, d_model), lambda i: (i, 0)), pl.BlockSpec((d_model, n_col), lambda i: (0, 0)),
                  pl.BlockSpec((rows, stats.shape[1]), lambda i: (i, 0)), pl.BlockSpec(gains.shape, lambda i: (0, 0))],
        out_specs=[spec] * 5,
        compiler_params=pltpu.CompilerParams(vmem_limit_bytes=60 * 2 ** 20),
        cost_estimate=pl.CostEstimate(flops=2 * n_dev * rows * d_model * n_col, bytes_accessed=80 * 2 ** 20, transcendentals=0),
        name='qkv_heads',
    )(h_all, w_pad, stats, gains)


def attention(q, k, v, d_o, slopes, head_dim, blk):
    n_batch, n_h, seq, _ = q.shape
    n_blk = seq // blk
    scale = head_dim ** -0.5

    def dot(a, b, ca, cb):
        return lax.dot_general(a, b, (((ca,), (cb,)), ((), ())), preferred_element_type=F32)

    def kernel(slope_ref, q_ref, k_ref, v_ref, do_ref, o_ref, dq_ref, dk_ref, dv_ref, s_ref, dk_acc, dv_acc):
        slope2 = slope_ref[pl.program_id(1)] * LOG2E
        dk_acc[...] = jnp.zeros_like(dk_acc)
        dv_acc[...] = jnp.zeros_like(dv_acc)
        key_iota = lax.broadcasted_iota(jnp.int32, (blk, LANES), 0)[:, :1]

        @pl.loop(0, n_blk)
        def _(i):
            q_rows = pl.ds(i * blk, blk)
            q_b = q_ref[0, 0, q_rows, :]
            do_b = do_ref[0, 0, q_rows, :]

            def score(j, diag):
                rows = pl.ds(j * blk, blk)
                s = dot(k_ref[0, 0, rows, :], q_b, 1, 1) * (scale * LOG2E)
                s = s + (key_iota + (j - i) * blk).astype(F32) * slope2
                if diag:
                    key_pos = lax.broadcasted_iota(jnp.int32, (blk, blk), 0)
                    q_pos = lax.broadcasted_iota(jnp.int32, (blk, blk), 1)
                    s = jnp.where(key_pos <= q_pos, s, -1e30)
                s_ref[rows, :] = s
                return jnp.max(s, axis=0, keepdims=True)

            top = score(i, True)
            top = lax.fori_loop(0, i, lambda j, m: jnp.maximum(m, score(j, False)), top)

            def weigh(j, carry):
                total, out_t = carry
                rows = pl.ds(j * blk, blk)
                w = jnp.exp2(s_ref[rows, :] - top)
                s_ref[rows, :] = w
                out_t = out_t + dot(v_ref[0, 0, rows, :], w.astype(BF16), 0, 0)
                return total + jnp.sum(w, axis=0, keepdims=True), out_t

            total, out_t = lax.fori_loop(0, i + 1, weigh, (jnp.zeros((1, blk), F32), jnp.zeros((LANES, blk), F32)))
            inv = 1.0 / total
            out_b = (out_t * inv).T.astype(BF16)
            o_ref[0, 0, q_rows, :] = out_b
            delta = jnp.sum((out_b.astype(F32) * do_b.astype(F32)).T, axis=0, keepdims=True)

            def back(j, dq_t):
                rows = pl.ds(j * blk, blk)
                k_b = k_ref[0, 0, rows, :]
                d_p = dot(v_ref[0, 0, rows, :], do_b, 1, 1)
                p = s_ref[rows, :] * inv
                dv_acc[rows, :] += dot(p.astype(BF16), do_b, 1, 0)
                d_s = (p * (d_p - delta)).astype(BF16)
                dk_acc[rows, :] += dot(d_s, q_b, 1, 0)
                return dq_t + dot(k_b, d_s, 0, 0)

            dq_t = lax.fori_loop(0, i + 1, back, jnp.zeros((LANES, blk), F32))
            dq_ref[0, 0, q_rows, :] = (dq_t * scale).T.astype(BF16)

        dk_ref[0, 0] = (dk_acc[...] * scale).astype(BF16)
        dv_ref[0, 0] = dv_acc[...].astype(BF16)

    spec = pl.BlockSpec((1, 1, seq, LANES), lambda b, n: (b, n, 0, 0))
    flops = 6 * 2 * n_batch * n_h * seq * seq * LANES
    return pl.pallas_call(
        kernel,
        grid=(n_batch, n_h),
        out_shape=[jax.ShapeDtypeStruct(q.shape, BF16)] * 4,
        in_specs=[pl.BlockSpec(memory_space=pltpu.SMEM)] + [spec] * 4,
        out_specs=[spec] * 4,
        scratch_shapes=[pltpu.VMEM((seq, blk), F32), pltpu.VMEM((seq, LANES), F32), pltpu.VMEM((seq, LANES), F32)],
        compiler_params=pltpu.CompilerParams(vmem_limit_bytes=60 * 2 ** 20),
        cost_estimate=pl.CostEstimate(flops=flops, bytes_accessed=40 * 2 ** 20, transcendentals=n_batch * n_h * seq * seq // 2),
        name='attention',
    )(slopes, q, k, v, d_o)


def place_columns(gathered, group):
    n_dev, parts, width, d_in = gathered.shape
    mb = 512 if d_in % 512 == 0 else d_in

    def kernel(x_ref, o_ref):
        o_ref[...] = x_ref[...].reshape(group * width, mb).T

    n_grp = n_dev // group
    return pl.pallas_call(
        kernel,
        grid=(parts, n_grp, d_in // mb),
        out_shape=jax.ShapeDtypeStruct((d_in, parts * n_dev * width), gathered.dtype),
        in_specs=[pl.BlockSpec((group, 1, width, mb), lambda p, g, m: (g, p, 0, m))],
        out_specs=pl.BlockSpec((mb, group * width), lambda p, g, m: (m, p * n_grp + g)),
        compiler_params=pltpu.CompilerParams(vmem_limit_bytes=40 * 2 ** 20),
        cost_estimate=pl.CostEstimate(flops=2 * gathered.size, bytes_accessed=8 * gathered.size, transcendentals=0),
        name='place_columns',
    )(gathered)


def solution(mesh):
    n_dev = mesh.shape['sp']
    seq_spec = P(None, 'sp', None)
    rep_spec = P()

    def local_step(x, ln1_w, w_qkv, q_ln_w, k_ln_w, w_out, grad_y):
        n_batch, tok, d_model = x.shape
        n_heads, head_dim = q_ln_w.shape
        n_h = n_heads // n_dev
        width = n_h * head_dim
        seq = tok * n_dev
        rows = n_batch * tok
        me = lax.axis_index('sp')
        slopes = lax.dynamic_slice_in_dim(alibi_slopes(n_heads), me * n_h, n_h)

        def pad_lanes(a):
            return jnp.pad(a, ((0, 0),) * (a.ndim - 1) + ((0, LANES - head_dim),))

        x_flat = x.reshape(rows, d_model).astype(F32)
        gy = grad_y.reshape(rows, d_model)
        h_f32, ln1_pull = jax.vjp(layer_norm, x_flat, ln1_w.astype(F32))
        h_loc = h_f32.astype(BF16)
        h_all = lax.all_gather(h_loc, 'sp', axis=0, tiled=True)

        qk_raw = jnp.dot(h_loc, w_qkv[:, :2 * d_model], preferred_element_type=F32)
        stats_loc = jnp.stack(row_stats(qk_raw[:, :d_model]) + row_stats(qk_raw[:, d_model:]))
        stats = exchange(stats_loc, n_dev)
        d_o = jnp.einsum('te,nde->ntd', gy, w_out.reshape(n_dev, width, d_model), preferred_element_type=F32).astype(BF16)
        d_o = lax.all_to_all(d_o, 'sp', 0, 0, tiled=True)
        d_o = d_o.reshape(n_dev, n_batch, tok, n_h, head_dim).transpose(1, 3, 0, 2, 4).reshape(n_batch, n_h, seq, head_dim)
        d_o = pad_lanes(d_o)
        slices = [lax.dynamic_slice_in_dim(w_qkv, p * d_model + me * width, width, axis=1) for p in range(3)]
        w_pad = jnp.concatenate([pad_lanes(s[:, n * head_dim:(n + 1) * head_dim]) for s in slices for n in range(n_h)], axis=1)
        gain_q = pad_lanes(lax.dynamic_slice_in_dim(q_ln_w, me * n_h, n_h).astype(F32))
        gain_k = pad_lanes(lax.dynamic_slice_in_dim(k_ln_w, me * n_h, n_h).astype(F32))
        stats_rows = stats.transpose(0, 2, 1).reshape(n_dev * rows, 4)

        q, k, v, hat_q, hat_k = qkv_heads(h_all, w_pad, stats_rows, jnp.concatenate([gain_q, gain_k]), n_dev, n_batch, tok, seq)
        gy_late, h_all = lax.optimization_barrier((gy, h_all))
        gy_all = lax.all_gather(gy_late, 'sp', axis=0, tiled=True)
        o, d_q, d_k, d_v = attention(q, k, v, d_o, slopes, head_dim, math.gcd(seq, 512))

        rstd = stats.reshape(n_dev, 4, n_batch, tok).transpose(1, 2, 0, 3).reshape(4, n_batch, seq)
        dq32, dk32 = d_q.astype(F32), d_k.astype(F32)
        gq = dq32 * gain_q[None, :, None, :]
        gk = dk32 * gain_k[None, :, None, :]
        part = jnp.stack([jnp.sum(gq, (1, 3)), jnp.sum(gq * hat_q, (1, 3)), jnp.sum(gk, (1, 3)), jnp.sum(gk * hat_k, (1, 3))])
        full = jnp.sum(exchange(part.reshape(-1, LANES), n_dev), axis=0).reshape(4, n_batch, seq) * (1.0 / d_model)

        def norm_back(g, hat, c1, c2, r):
            e = lambda a: a[:, None, :, None]
            return (e(r) * (g - e(c1) - hat * e(c2))).astype(BF16)

        dq_raw = norm_back(gq, hat_q, full[0], full[1], rstd[1])
        dk_raw = norm_back(gk, hat_k, full[2], full[3], rstd[3])
        grad_q_ln = jnp.sum(dq32 * hat_q, (0, 2))[:, :head_dim]
        grad_k_ln = jnp.sum(dk32 * hat_k, (0, 2))[:, :head_dim]

        def to_rows(a):
            a = a[..., :head_dim].reshape(n_batch, n_h, n_dev, tok, head_dim)
            return a.transpose(2, 0, 3, 1, 4).reshape(n_dev, rows, width)

        back = jnp.concatenate([to_rows(a) for a in (dq_raw, dk_raw, d_v, o)], axis=-1)
        back_flat = back.reshape(n_dev * rows, 4 * width)
        tok_side = lax.all_to_all(back, 'sp', 0, 0, tiled=True)
        dw_out = lax.dot_general(back_flat[:, 3 * width:], gy_all, (((0,), (0,)), ((), ())), preferred_element_type=F32)
        dw_qkv_t = lax.dot_general(back_flat[:, :3 * width], h_all, (((0,), (0,)), ((), ())), preferred_element_type=F32)
        grad_w_out = lax.all_gather(dw_out, 'sp', axis=0, tiled=True)
        dw_all = lax.all_gather(dw_qkv_t, 'sp', axis=0, tiled=True)
        grad_w_qkv = place_columns(dw_all.reshape(n_dev, 3, width, d_model), 4)

        o_tok = tok_side[:, :, 3 * width:].transpose(1, 0, 2).reshape(rows, d_model)
        y = (jnp.dot(o_tok, w_out, preferred_element_type=F32) + x_flat).astype(BF16)
        d_qkv = tok_side[:, :, :3 * width].reshape(n_dev, rows, 3, width).transpose(1, 2, 0, 3).reshape(rows, 3 * d_model)
        d_h = lax.dot_general(d_qkv, w_qkv, (((1,), (1,)), ((), ())), preferred_element_type=F32).astype(BF16)
        d_x_norm, grad_ln1 = ln1_pull(d_h.astype(F32))
        grad_x = (d_x_norm + gy.astype(F32)).astype(BF16)

        small = jnp.concatenate([grad_ln1, grad_q_ln.reshape(-1), grad_k_ln.reshape(-1)])
        n_small = small.shape[0]
        pad = -n_small % (8 * LANES)
        small_all = exchange(jnp.pad(small, (0, pad)).reshape(-1, LANES), n_dev).reshape(n_dev, n_small + pad)
        grad_ln1 = jnp.sum(small_all[:, :d_model], axis=0)
        grad_q_ln = small_all[:, d_model:d_model + width].reshape(n_heads, head_dim)
        grad_k_ln = small_all[:, d_model + width:d_model + 2 * width].reshape(n_heads, head_dim)
        shape = (n_batch, tok, d_model)
        return y.reshape(shape), grad_x.reshape(shape), grad_ln1, grad_w_qkv, grad_q_ln, grad_k_ln, grad_w_out

    return jax.shard_map(local_step, mesh=mesh, in_specs=(seq_spec, rep_spec, rep_spec, rep_spec, rep_spec, rep_spec, seq_spec), out_specs=(seq_spec, seq_spec, rep_spec, rep_spec, rep_spec, rep_spec, rep_spec), check_vma=False)
```

time: 2250 us -> 1130 us (0.50)
  waiting for transfers between devices: 1030 us -> 410 us
  matrix products: 672 us -> 118 us
  Pallas kernels: 0 us -> 329 us
  local copies, waits for them, and re-layouts: 276 us -> 160 us
  other arithmetic: 157 us -> 77.5 us
  loops' own time: 43.1 us -> 0 us
  blocking collectives: 34.8 us -> 0 us
    psum x1 -> x0, waiting for transfers between devices: 812 us -> none  [local_step(): lax.psum((grad_ln1, grad_w_qkv, grad_q_ln.reshape(n_heads, head_dim), gra...]
    dot_general x62 -> x6, matrix products: 672 us -> 118 us  [the longest x1 27.8 us: local_step(): lax.dot_general(back_flat[:, :3 * width], h_all, (((0,), (0,)), ((), ()))...]
    pallas_call x0 -> x6, Pallas kernels: none -> 329 us  [the longest x1 126 us: attention(): pl.pallas_call(kernel, grid=(n_batch, n_h), out_shape=[jax.ShapeDtypeStru...]
    all_gather x0 -> x4, waiting for transfers between devices: none -> 217 us  [the longest x1 161 us: local_step(): h_all = lax.all_gather(h_loc, 'sp', axis=0, tiled=True)]
    another operation x7 -> x0, local copies, waits for them, and re-layouts: 54.7 us -> none  [the longest x2 36.1 us: local_step(): jnp.stack([d_q, d_k.astype(jnp.bfloat16), d_v.astype(jnp.bfloat16)])]
    unnamed x81 -> x52, local copies, waits for them, and re-layouts: 77.4 us -> 30.6 us
    all_to_all x5 -> x0, local copies, waits for them, and re-layouts: 44.1 us -> none  [the longest x1 20.2 us: local_step(): d_qkv_tok = lax.all_to_all(d_qkv_head, 'sp', 2, 3, tiled=True)]
    another operation x2 -> x0, loops' own time: 43.1 us -> none  [the longest x1 21.8 us: attn_backward(): lax.scan(one_block, (zero_acc, zero_acc), jnp.arange(n_blk))]
  transfers between devices with their start and end apart: 5 -> 6, of which waited for: 3 -> 3; matrix products, arithmetic and copies ran while one was open for 27% -> 27% of each run, Pallas kernels for 0% -> 22%
where the time goes in v1:
time: 1130 us; the launch traced here: 1110 us
  waiting for transfers between devices  410 us (36%)
  Pallas kernels  329 us (29%)
  local copies, waits for them, and re-layouts  160 us (14%)
  matrix products  118 us (10%)
  other arithmetic  77.5 us (7%)
  between operations  14.3 us (1%)
    all_to_all x1, waiting for transfers between devices, local_step(): tok_side = lax.all_to_all(back, 'sp', 0, 0, tiled=True)  193 us
    all_gather x1, waiting for transfers between devices, local_step(): h_all = lax.all_gather(h_loc, 'sp', axis=0, tiled=True)  161 us
    pallas_call x1, Pallas kernels, attention(): pl.pallas_call(kernel, grid=(n_batch, n_h), out_shape=[jax.ShapeDtypeStru...  126 us
    pallas_call x1, Pallas kernels, place_columns(): pl.pallas_call(kernel, grid=(parts, n_grp, d_in // mb), out_shape=jax.Sha...  81.4 us
    pallas_call x3, Pallas kernels, exchange(): pl.pallas_call(kernel, out_shape=jax.ShapeDtypeStruct((n_dev,) + block.sh...  80.4 us
    all_gather x1, waiting for transfers between devices, local_step(): dw_all = lax.all_gather(dw_qkv_t, 'sp', axis=0, tiled=True)  55.6 us
    pallas_call x1, Pallas kernels, qkv_heads(): pl.pallas_call(kernel, grid=(n_dev,), out_shape=[jax.ShapeDtypeStruct(sha...  41.3 us
    unnamed x52, local copies, waits for them, and re-layouts  30.6 us
  transfers between devices with their start and end apart: 6, of which 3 were waited for; matrix products, arithmetic and copies ran while one was open for 27% of the time, Pallas kernels for 22%

profile of v1, /device:TPU:1, one launch (start us, length us, event | category | flops | bytes accessed | tf_op | source)
XLA Modules:
  0.0 1114.9 jit_solution(16064072641650425914)
XLA Ops:
  16.3 161.2 %all-gather.5.cloned.1.call-done.h_ref = bf16[8192,2560]{1,0:T(8,128)(2,1)} async-done(((bf16[512,2560]{1,0:T(8,128)(2,1)}), bf16[8192,2560]{1,0:T(8,128)(2,1)}) %all-gather.5.cloned.1.call-update) | async-done | bytes 41943056 | tf_op jit(solution)/shard_map/all_gather | solution.py:220
  177.6 11.1 convert_bitcast_fusion
  193.8 21.7 %fusion = f32[512,5120]{1,0:T(8,128)} fusion(bf16[512,2560]{1,0:T(8,128)(2,1)} %fusion.23, bf16[2560,7680]{1,0:T(8,128)(2,1)} %param.9), kind=kOutput, calls=%fused_computation | convolution fusion | flops 13421772800 | bytes 39321600 | tf_op jit(solution)/shard_map/dot_general | solution.py:222
  231.6 11.8 %exchange.3 = f32[16,4,512]{2,1,0:T(4,128)} custom-call(f32[4,512]{1,0:T(4,128)} %pad_maximum_fusion.2.x_ref), custom_call_target="tpu_custom_call" | custom-call | tf_op jit(solution)/shard_map/exchange/pallas_call | solution.py:54
  259.9 7.0 copy.17
  272.0 41.3 %qkv_heads.1 = (bf16[4,2,2048,128]{3,2,1,0:T(8,128)(2,1)}, bf16[4,2,2048,128]{3,2,1,0:T(8,128)(2,1)}, bf16[4,2,2048,128]{3,2,1,0:T(8,128)(2,1)}, f32[4,2,2048,128]{3,2,1,0:T(8,128)}, f32[4,2,2048,128]{3,2,1,0:T(8,128)}) custom-call(bf16[8192,2560]{1,0:T(8,128)(2,1)} %all-gather.5.cloned.1.call-done.h_ref, ...), custom_call_target="tpu_custom_call" | custom-call | flops 32212254720 | bytes 83886080 | tf_op jit(solution)/shard_map/qkv_heads/pallas_call | solution.py:86
  313.2 125.8 %attention.1 = (bf16[4,2,2048,128]{3,2,1,0:T(8,128)(2,1)}, bf16[4,2,2048,128]{3,2,1,0:T(8,128)(2,1)}, bf16[4,2,2048,128]{3,2,1,0:T(8,128)(2,1)}, bf16[4,2,2048,128]{3,2,1,0:T(8,128)(2,1)}) custom-call(f32[2]{0:T(128)} %dynamic_slice.18.slope_ref, bf16[4,2,2048,128]{3,2,1,0:T(8,128)(2,1)} %get-tuple-element.18.q_ref, ...), custom_call_target="tpu_custom_call" | custom-call | flops 51539607552 | bytes 41943040 | tf_op jit(solution)/shard_map/attention/pallas_call | solution.py:165
  448.6 18.5 %fusion.37 = f32[160,2560]{1,0:T(8,128)} fusion(bf16[8192,160]{0,1:T(8,128)(2,1)} %concatenate.32, bf16[8192,2560]{1,0:T(8,128)(2,1)} %all-gather.9.cloned.1.call-done), kind=kOutput, calls=%fused_computation.95 | convolution fusion | flops 6710886400 | bytes 46202880 | tf_op jit(solution)/shard_map/dot_general | solution.py:263
  467.3 10.0 fusion.3
  486.3 46.6 %exchange.4 = f32[16,256,128]{2,1,0:T(8,128)} custom-call(f32[256,128]{1,0:T(8,128)} %reshape.246.x_ref), custom_call_target="tpu_custom_call" | custom-call | tf_op jit(solution)/shard_map/exchange/pallas_call | solution.py:54
  544.2 8.6 fusion.6
  562.3 8.5 fusion.9
  580.3 27.8 %fusion.10 = f32[480,2560]{1,0:T(8,128)} fusion(bf16[8192,2560]{1,0:T(8,128)(2,1)} %all-gather.5.cloned.1.call-done.h_ref, bf16[8192,160]{0,1:T(8,128)(2,1)} %concatenate.30, bf16[8192,160]{0,1:T(8,128)(2,1)} %concatenate.29, bf16[8192,160]{0,1:T(8,128)(2,1)} %concatenate.28), kind=kOutput, calls=%fused_computation.21 | convolution fusion | flops 20156252160 | bytes 54722560 | tf_op jit(solution)/shard_map/dot_general | solution.py:264
  628.9 6.9 copy.27
  654.9 11.8 %pad_maximum_fusion = bf16[16,512,640]{1,2,0:T(8,128)(2,1)} fusion(bf16[16,512,160]{1,2,0:T(8,128)(2,1)S(1)} %reshape.254, bf16[16,512,160]{1,2,0:T(8,128)(2,1)} %reshape.252, bf16[16,512,160]{1,2,0:T(8,128)(2,1)} %reshape.250, bf16[16,512,160]{1,2,0:T(8,128)(2,1)} %reshape.248), kind=kLoop, calls=%fused_computation.6 | loop fusion | flops 41943040 | bytes 20971520 | tf_op jit(solution)/shard_map/concatenate | solution.py:260
  670.8 193.0 %all-to-all-done.1 = bf16[16,512,640]{1,2,0:T(8,128)(2,1)} async-done(((bf16[16,512,640]{1,2,0:T(8,128)(2,1)}), bf16[16,512,640]{1,2,0:T(8,128)(2,1)}, u32[]{:S(2)}, u32[]{:S(2)}) %all-to-all-start.1) | async-done | bytes 10485792 | tf_op jit(solution)/shard_map/all_to_all | solution.py:262
  863.8 7.1 slice.129
  870.9 7.5 copy.26
  878.4 27.5 %fusion.18 = (f32[512]{0:T(512)S(1)}, bf16[512,2560]{1,0:T(8,128)(2,1)S(1)}) fusion(bf16[4,128,2560]{2,1,0:T(8,128)(2,1)S(1)} %copy-done.1, f32[2560]{0:T(1024)S(1)} %copy-done.10, f32[512]{0:T(512)S(1)} %copy-done.12, bf16[512,7680]{0,1:T(8,128)(2,1)} %bitcast.139, bf16[2560,7680]{1,0:T(8,128)(2,1)} %param.9), kind=kOutput, calls=%fused_computation.32 | convolution fusion | flops 20141834240 | bytes 52443136 | tf_op jit(solution)/shard_map/dot_general | solution.py:272
  910.8 21.9 %exchange.5 = f32[16,24,128]{2,1,0:T(8,128)} custom-call(f32[24,128]{1,0:T(8,128)} %pad_bitcast_fusion.x_ref), custom_call_target="tpu_custom_call" | custom-call | tf_op jit(solution)/shard_map/exchange/pallas_call | solution.py:54
  942.3 11.3 %fusion.26 = bf16[512,2560]{1,0:T(8,128)(2,1)} fusion(bf16[4,128,2560]{2,1,0:T(8,128)(2,1)S(1)} %copy-done.1, bf16[512,2560]{0,1:T(8,128)(2,1)S(1)} %bitcast.141, bf16[2560,2560]{1,0:T(8,128)(2,1)} %param.12), kind=kOutput, calls=%fused_computation.44 | convolution fusion | flops 6714818560 | bytes 20971520 | tf_op jit(solution)/shard_map/dot_general | solution.py:270
  953.6 55.6 %all-gather.7.cloned.1.call-done = f32[7680,2560]{1,0:T(8,128)} async-done(((f32[480,2560]{1,0:T(8,128)}), f32[7680,2560]{1,0:T(8,128)}) %all-gather.7.cloned.1.call-update) | async-done | bytes 78643216 | tf_op jit(solution)/shard_map/all_gather | solution.py:266
  1009.2 81.4 %place_columns.1 = f32[2560,7680]{1,0:T(8,128)} custom-call(f32[16,3,160,2560]{3,2,1,0:T(8,128)} %bitcast.42.x_ref), custom_call_target="tpu_custom_call" | custom-call | flops 39321600 | bytes 157286400 | tf_op jit(solution)/shard_map/place_columns/pallas_call | solution.py:186
  1090.6 17.5 %copy.40 = f32[2560,2560]{1,0:T(8,128)} copy(f32[2560,2560]{1,0:T(8,128)} %all-gather.11.cloned.1.call-done) | data formatting | bytes 52428800
  (131 shorter events, 158.9 us)
Async XLA Ops:
  7.2 6.8 copy-start
  7.2 170.4 %all-gather.5.cloned.1.call-start = ((), (), s32[]{:S(2)}) async-start(), calls=%async_computation.2 | async-start | bytes 44564480 | tf_op jit(solution)/shard_map/all_gather | solution.py:220
  8.1 5.3 copy-start.9
  10.2 3.2 copy-start.11
  16.3 161.3 %copy-start.5 = (bf16[4,128,2560]{2,1,0:T(8,128)(2,1)S(1)}, bf16[4,128,2560]{2,1,0:T(8,128)(2,1)}, u32[]{:S(2)}) copy-start(bf16[4,128,2560]{2,1,0:T(8,128)(2,1)} %param.13) | copy-start | bytes 7864324
  16.3 432.3 %all-gather.9.cloned.1.call-start = ((), (), s32[]{:S(2)}) async-start(), calls=%async_computation.4 | async-start | bytes 44564480 | tf_op jit(solution)/shard_map/all_gather | solution.py:237
  188.7 68.5 %all-to-all-start = ((bf16[16,512,160]{1,2,0:T(8,128)(2,1)}), bf16[16,512,160]{1,2,0:T(8,128)(2,1)S(1)}, u32[]{:S(2)}, u32[]{:S(2)}) async-start(bf16[16,512,160]{1,2,0:T(8,128)(2,1)} %convert_bitcast_fusion), calls=%async_computation | async-start | bytes 5242880 | tf_op jit(solution)/shard_map/all_to_all | solution.py:226
  191.3 762.2 %all-gather.11.cloned.1.call-start = ((), (), s32[]{:S(2)}) async-start(), calls=%async_computation.5 | async-start | bytes 27852800 | tf_op jit(solution)/shard_map/all_gather | solution.py:265
  215.5 7.0 copy-start.2
  222.5 5.9 copy-start.17
  448.6 18.6 %copy-start.8 = (f32[16,4,512]{2,1,0:T(4,128)S(1)}, f32[16,4,512]{2,1,0:T(4,128)}, u32[]{:S(2)}) copy-start(f32[16,4,512]{2,1,0:T(4,128)} %exchange.3) | copy-start | bytes 393220
  448.6 18.7 %copy-start.21 = (f32[2,128]{1,0:T(2,128)S(1)}, f32[2,128]{1,0:T(2,128)}, u32[]{:S(2)}) copy-start(f32[2,128]{1,0:T(2,128)} %copy-done.20) | copy-start | bytes 3076
  467.1 542.2 %all-gather.7.cloned.1.call-start = ((), (), s32[]{:S(2)}) async-start(), calls=%async_computation.3 | async-start | bytes 83558400 | tf_op jit(solution)/shard_map/all_gather | solution.py:266
  467.2 10.1 slice-start
  467.2 10.1 slice-start.1
  467.3 11.3 %copy-start.7 = (bf16[4,2,2048,128]{3,2,1,0:T(8,128)(2,1)S(1)}, bf16[4,2,2048,128]{3,2,1,0:T(8,128)(2,1)}, u32[]{:S(2)}) copy-start(bf16[4,2,2048,128]{3,2,1,0:T(8,128)(2,1)} %get-tuple-element.21) | copy-start | bytes 12582916
  467.3 11.3 %copy-start.19 = (f32[2,128]{1,0:T(2,128)S(1)}, f32[2,128]{1,0:T(2,128)}, u32[]{:S(2)}) copy-start(f32[2,128]{1,0:T(2,128)} %copy-done.18) | copy-start | bytes 3076
  666.7 197.1 %all-to-all-start.1 = ((bf16[16,512,640]{1,2,0:T(8,128)(2,1)}), bf16[16,512,640]{1,2,0:T(8,128)(2,1)}, u32[]{:S(2)}, u32[]{:S(2)}) async-start(bf16[16,512,640]{1,2,0:T(8,128)(2,1)} %pad_maximum_fusion), calls=%async_computation.1 | async-start | bytes 20971520 | tf_op jit(solution)/shard_map/all_to_all | solution.py:262
  870.9 7.5 copy-start.1
  870.9 7.5 copy-start.10
  870.9 7.5 copy-start.12
  878.4 27.6 %copy-start.16 = (f32[4,128]{1,0:T(4,128)S(1)}, f32[4,128]{1,0:T(4,128)}, u32[]{:S(2)}) copy-start(f32[4,128]{1,0:T(4,128)} %copy-done.15) | copy-start | bytes 6148
  878.4 29.0 %copy-start.14 = (f32[512]{0:T(512)S(1)}, f32[512]{0:T(512)}, u32[]{:S(2)}) copy-start(f32[512]{0:T(512)} %copy-done.13) | copy-start | bytes 6148
  935.1 3.3 copy-start.6
  (6 other events, 6.4 us)
Sparse Core Ops, SparseCore 0:
  16.4 161.0 all-gather.4
  179.8 186.4 all-gather.8
  467.2 124.9 all-gather.10
  608.3 400.9 all-gather.6

commit v2 on v1

--- a/solution.py
+++ b/solution.py
@@ -1,4 +1,3 @@
-import functools
 import math
 import jax
 import jax.numpy as jnp
@@ -36,16 +35,20 @@
     return mean[..., 0], lax.rsqrt(var_val + 1e-5)
 
 
-def exchange(block, n_dev):
+def exchange(block, n_dev, scatter=False):
+    shape = block.shape[1:] if scatter else block.shape
+
     def kernel(x_ref, o_ref, loc_sem, send_sem, recv_sem):
         me = lax.axis_index('sp')
-        own = pltpu.make_async_copy(x_ref, o_ref.at[me], loc_sem)
+        src = (lambda dev: x_ref.at[dev]) if scatter else (lambda dev: x_ref)
+        own = pltpu.make_async_copy(src(me), o_ref.at[me], loc_sem)
         own.start()
         copies = []
         for step in range(1, n_dev):
+            peer = lax.rem(me + step, n_dev)
             copies.append(pltpu.make_async_remote_copy(
-                src_ref=x_ref, dst_ref=o_ref.at[me], send_sem=send_sem.at[step], recv_sem=recv_sem.at[step],
-                device_id=(lax.rem(me + step, n_dev),), device_id_type=MESH))
+                src_ref=src(peer), dst_ref=o_ref.at[me], send_sem=send_sem.at[step], recv_sem=recv_sem.at[step],
+                device_id=(peer,), device_id_type=MESH))
             copies[-1].start()
         own.wait()
         for copy in copies:
@@ -53,12 +56,12 @@
 
     return pl.pallas_call(
         kernel,
-        out_shape=jax.ShapeDtypeStruct((n_dev,) + block.shape, block.dtype),
+        out_shape=jax.ShapeDtypeStruct((n_dev,) + shape, block.dtype),
         in_specs=[pl.BlockSpec(memory_space=pl.ANY)],
         out_specs=pl.BlockSpec(memory_space=pl.ANY),
         scratch_shapes=[pltpu.SemaphoreType.DMA, pltpu.SemaphoreType.DMA((n_dev,)), pltpu.SemaphoreType.DMA((n_dev,))],
         compiler_params=pltpu.CompilerParams(has_side_effects=True),
-        name='exchange',
+        name='scatter_rows' if scatter else 'exchange',
     )(block)
 
 
@@ -101,61 +104,56 @@
     n_blk = seq // blk
     scale = head_dim ** -0.5
 
-    def dot(a, b, ca, cb):
-        return lax.dot_general(a, b, (((ca,), (cb,)), ((), ())), preferred_element_type=F32)
-
-    def kernel(slope_ref, q_ref, k_ref, v_ref, do_ref, o_ref, dq_ref, dk_ref, dv_ref, s_ref, dk_acc, dv_acc):
+    def dot(a, b):
+        return jnp.dot(a, b, preferred_element_type=F32)
+
+    def kernel(slope_ref, q_ref, k_ref, v_ref, do_ref, o_ref, dq_ref, dk_ref, dv_ref, w_ref, dk_acc, dv_acc, kt_ref, vt_ref):
         slope2 = slope_ref[pl.program_id(1)] * LOG2E
         dk_acc[...] = jnp.zeros_like(dk_acc)
         dv_acc[...] = jnp.zeros_like(dv_acc)
+        kt_ref[...] = k_ref[0, 0].T
+        vt_ref[...] = v_ref[0, 0].T
         key_iota = lax.broadcasted_iota(jnp.int32, (blk, LANES), 0)[:, :1]
-
-        @pl.loop(0, n_blk)
-        def _(i):
-            q_rows = pl.ds(i * blk, blk)
-            q_b = q_ref[0, 0, q_rows, :]
-            do_b = do_ref[0, 0, q_rows, :]
-
-            def score(j, diag):
-                rows = pl.ds(j * blk, blk)
-                s = dot(k_ref[0, 0, rows, :], q_b, 1, 1) * (scale * LOG2E)
+        blocks = [pl.ds(j * blk, blk) for j in range(n_blk)]
+
+        for i in range(n_blk):
+            q_b = q_ref[0, 0, blocks[i], :]
+            do_b = do_ref[0, 0, blocks[i], :]
+            q_t = q_b.T
+            do_t = do_b.T
+            top = None
+            for j in range(i, -1, -1):
+                s = dot(k_ref[0, 0, blocks[j], :], q_t) * (scale * LOG2E)
                 s = s + (key_iota + (j - i) * blk).astype(F32) * slope2
-                if diag:
+                if i == j:
                     key_pos = lax.broadcasted_iota(jnp.int32, (blk, blk), 0)
                     q_pos = lax.broadcasted_iota(jnp.int32, (blk, blk), 1)
                     s = jnp.where(key_pos <= q_pos, s, -1e30)
-                s_ref[rows, :] = s
-                return jnp.max(s, axis=0, keepdims=True)
-
-            top = score(i, True)
-            top = lax.fori_loop(0, i, lambda j, m: jnp.maximum(m, score(j, False)), top)
-
-            def weigh(j, carry):
-                total, out_t = carry
-                rows = pl.ds(j * blk, blk)
-                w = jnp.exp2(s_ref[rows, :] - top)
-                s_ref[rows, :] = w
-                out_t = out_t + dot(v_ref[0, 0, rows, :], w.astype(BF16), 0, 0)
-                return total + jnp.sum(w, axis=0, keepdims=True), out_t
-
-            total, out_t = lax.fori_loop(0, i + 1, weigh, (jnp.zeros((1, blk), F32), jnp.zeros((LANES, blk), F32)))
+                w_ref[blocks[j], :] = s
+                peak = jnp.max(s, axis=0, keepdims=True)
+                top = peak if top is None else jnp.maximum(top, peak)
+
+            total = jnp.zeros((1, blk), F32)
+            out_t = jnp.zeros((LANES, blk), F32)
+            for j in range(i + 1):
+                w = jnp.exp2(w_ref[blocks[j], :] - top)
+                w_ref[blocks[j], :] = w
+                out_t = out_t + dot(vt_ref[:, blocks[j]], w.astype(BF16))
+                total = total + jnp.sum(w, axis=0, keepdims=True)
             inv = 1.0 / total
             out_b = (out_t * inv).T.astype(BF16)
-            o_ref[0, 0, q_rows, :] = out_b
+            o_ref[0, 0, blocks[i], :] = out_b
             delta = jnp.sum((out_b.astype(F32) * do_b.astype(F32)).T, axis=0, keepdims=True)
 
-            def back(j, dq_t):
-                rows = pl.ds(j * blk, blk)
-                k_b = k_ref[0, 0, rows, :]
-                d_p = dot(v_ref[0, 0, rows, :], do_b, 1, 1)
-                p = s_ref[rows, :] * inv
-                dv_acc[rows, :] += dot(p.astype(BF16), do_b, 1, 0)
+            dq_t = jnp.zeros((LANES, blk), F32)
+            for j in range(i + 1):
+                d_p = dot(v_ref[0, 0, blocks[j], :], do_t)
+                p = w_ref[blocks[j], :] * inv
+                dv_acc[blocks[j], :] += dot(p.astype(BF16), do_b)
                 d_s = (p * (d_p - delta)).astype(BF16)
-                dk_acc[rows, :] += dot(d_s, q_b, 1, 0)
-                return dq_t + dot(k_b, d_s, 0, 0)
-
-            dq_t = lax.fori_loop(0, i + 1, back, jnp.zeros((LANES, blk), F32))
-            dq_ref[0, 0, q_rows, :] = (dq_t * scale).T.astype(BF16)
+                dk_acc[blocks[j], :] += dot(d_s, q_b)
+                dq_t = dq_t + dot(kt_ref[:, blocks[j]], d_s)
+            dq_ref[0, 0, blocks[i], :] = (dq_t * scale).T.astype(BF16)
 
         dk_ref[0, 0] = (dk_acc[...] * scale).astype(BF16)
         dv_ref[0, 0] = dv_acc[...].astype(BF16)
@@ -168,31 +166,114 @@
         out_shape=[jax.ShapeDtypeStruct(q.shape, BF16)] * 4,
         in_specs=[pl.BlockSpec(memory_space=pltpu.SMEM)] + [spec] * 4,
         out_specs=[spec] * 4,
-        scratch_shapes=[pltpu.VMEM((seq, blk), F32), pltpu.VMEM((seq, LANES), F32), pltpu.VMEM((seq, LANES), F32)],
+        scratch_shapes=[pltpu.VMEM((seq, blk), F32), pltpu.VMEM((seq, LANES), F32), pltpu.VMEM((seq, LANES), F32),
+                        pltpu.VMEM((LANES, seq), BF16), pltpu.VMEM((LANES, seq), BF16)],
         compiler_params=pltpu.CompilerParams(vmem_limit_bytes=60 * 2 ** 20),
         cost_estimate=pl.CostEstimate(flops=flops, bytes_accessed=40 * 2 ** 20, transcendentals=n_batch * n_h * seq * seq // 2),
         name='attention',
     )(slopes, q, k, v, d_o)
 
 
-def place_columns(gathered, group):
+def place_columns(buf, gathered, first, n_part, group):
     n_dev, parts, width, d_in = gathered.shape
     mb = 512 if d_in % 512 == 0 else d_in
-
-    def kernel(x_ref, o_ref):
-        o_ref[...] = x_ref[...].reshape(group * width, mb).T
-
     n_grp = n_dev // group
+
+    def kernel(x_ref, *refs):
+        refs[-1][...] = x_ref[...].reshape(group * width, mb).T
+
+    args = (gathered,) if buf is None else (gathered, buf)
     return pl.pallas_call(
         kernel,
         grid=(parts, n_grp, d_in // mb),
-        out_shape=jax.ShapeDtypeStruct((d_in, parts * n_dev * width), gathered.dtype),
-        in_specs=[pl.BlockSpec((group, 1, width, mb), lambda p, g, m: (g, p, 0, m))],
-        out_specs=pl.BlockSpec((mb, group * width), lambda p, g, m: (m, p * n_grp + g)),
+        out_shape=jax.ShapeDtypeStruct((d_in, n_part * n_dev * width), gathered.dtype),
+        in_specs=[pl.BlockSpec((group, 1, width, mb), lambda p, g, m: (g, p, 0, m))] + [pl.BlockSpec(memory_space=pl.ANY)] * (len(args) - 1),
+        out_specs=pl.BlockSpec((mb, group * width), lambda p, g, m: (m, (p + first) * n_grp + g)),
+        input_output_aliases={1: 0} if buf is not None else {},
         compiler_params=pltpu.CompilerParams(vmem_limit_bytes=40 * 2 ** 20),
         cost_estimate=pl.CostEstimate(flops=2 * gathered.size, bytes_accessed=8 * gathered.size, transcendentals=0),
         name='place_columns',
-    )(gathered)
+    )(*args)
+
+
+def head_grads(side, acts, n_dev, n_batch, tok, head_dim):
+    n_h = side.shape[1]
+    rows, d_model = n_batch * tok, acts.shape[-1]
+
+    def kernel(s_ref, a_ref, o_ref, acc):
+        step = pl.program_id(0)
+        lhs = jnp.concatenate([s_ref[:, n].reshape(rows, LANES) for n in range(n_h)], axis=1)
+        out = lax.dot_general(lhs, a_ref[...], (((0,), (0,)), ((), ())), preferred_element_type=F32)
+
+        @pl.when(step == 0)
+        def _():
+            acc[...] = out
+
+        @pl.when(step > 0)
+        def _():
+            acc[...] += out
+
+        @pl.when(step == n_dev - 1)
+        def _():
+            for n in range(n_h):
+                o_ref[n * head_dim:(n + 1) * head_dim, :] = acc[n * LANES:n * LANES + head_dim, :]
+
+    return pl.pallas_call(
+        kernel,
+        grid=(n_dev,),
+        out_shape=jax.ShapeDtypeStruct((n_h * head_dim, d_model), F32),
+        in_specs=[pl.BlockSpec((n_batch, n_h, tok, LANES), lambda i: (0, 0, i, 0)), pl.BlockSpec((rows, d_model), lambda i: (i, 0))],
+        out_specs=pl.BlockSpec((n_h * head_dim, d_model), lambda i: (0, 0)),
+        scratch_shapes=[pltpu.VMEM((n_h * LANES, d_model), F32)],
+        compiler_params=pltpu.CompilerParams(vmem_limit_bytes=50 * 2 ** 20),
+        cost_estimate=pl.CostEstimate(flops=2 * n_dev * rows * d_model * n_h * LANES, bytes_accessed=50 * 2 ** 20, transcendentals=0),
+        name='head_grads',
+    )(side, acts)
+
+
+def norm_back(d_q, d_k, hat_q, hat_k, d_v, o, cols, gains, acts, n_dev, n_batch, tok, head_dim):
+    n_h = d_q.shape[1]
+    rows, d_model = n_batch * tok, acts.shape[-1]
+    width = n_h * head_dim
+
+    def kernel(dq_ref, dk_ref, xq_ref, xk_ref, dv_ref, o_ref, c_ref, g_ref, a_ref, w_ref, b_ref, acc):
+        step = pl.program_id(0)
+        sides = []
+        for part, (d_ref, x_ref) in enumerate(((dq_ref, xq_ref), (dk_ref, xk_ref))):
+            r, c1, c2 = (c_ref[:, 3 * part + m:3 * part + m + 1] for m in range(3))
+            for n in range(n_h):
+                g = d_ref[:, n].reshape(rows, LANES).astype(F32) * g_ref[part * n_h + n:part * n_h + n + 1, :]
+                sides.append((r * (g - c1 - x_ref[:, n].reshape(rows, LANES) * c2)).astype(BF16))
+        out = lax.dot_general(jnp.concatenate(sides, axis=1), a_ref[...], (((0,), (0,)), ((), ())), preferred_element_type=F32)
+        sides += [ref[:, n].reshape(rows, LANES) for ref in (dv_ref, o_ref) for n in range(n_h)]
+        b_ref[0] = jnp.concatenate([a[:, :head_dim] for a in sides], axis=1)
+
+        @pl.when(step == 0)
+        def _():
+            acc[...] = out
+
+        @pl.when(step > 0)
+        def _():
+            acc[...] += out
+
+        @pl.when(step == n_dev - 1)
+        def _():
+            for n in range(2 * n_h):
+                w_ref[n * head_dim:(n + 1) * head_dim, :] = acc[n * LANES:n * LANES + head_dim, :]
+
+    heads = pl.BlockSpec((n_batch, n_h, tok, LANES), lambda i: (0, 0, i, 0))
+    return pl.pallas_call(
+        kernel,
+        grid=(n_dev,),
+        out_shape=[jax.ShapeDtypeStruct((2 * width, d_model), F32), jax.ShapeDtypeStruct((n_dev, rows, 4 * width), BF16)],
+        in_specs=[heads] * 6 + [pl.BlockSpec((rows, cols.shape[1]), lambda i: (i, 0)), pl.BlockSpec(gains.shape, lambda i: (0, 0)),
+                                pl.BlockSpec((rows, d_model), lambda i: (i, 0))],
+        out_specs=[pl.BlockSpec((2 * width, d_model), lambda i: (0, 0)), pl.BlockSpec((1, rows, 4 * width), lambda i: (i, 0, 0))],
+        scratch_shapes=[pltpu.VMEM((2 * n_h * LANES, d_model), F32)],
+        compiler_params=pltpu.CompilerParams(vmem_limit_bytes=60 * 2 ** 20),
+        cost_estimate=pl.CostEstimate(flops=4 * n_dev * rows * d_model * n_h * LANES, bytes_accessed=90 * 2 ** 20, transcendentals=0),
+        name='norm_back',
+    )(d_q, d_k, hat_q, hat_k, d_v, o, cols, gains, acts)
 
 
 def solution(mesh):
@@ -230,41 +311,40 @@
         w_pad = jnp.concatenate([pad_lanes(s[:, n * head_dim:(n + 1) * head_dim]) for s in slices for n in range(n_h)], axis=1)
         gain_q = pad_lanes(lax.dynamic_slice_in_dim(q_ln_w, me * n_h, n_h).astype(F32))
         gain_k = pad_lanes(lax.dynamic_slice_in_dim(k_ln_w, me * n_h, n_h).astype(F32))
+        gains = jnp.concatenate([gain_q, gain_k])
         stats_rows = stats.transpose(0, 2, 1).reshape(n_dev * rows, 4)
 
-        q, k, v, hat_q, hat_k = qkv_heads(h_all, w_pad, stats_rows, jnp.concatenate([gain_q, gain_k]), n_dev, n_batch, tok, seq)
-        gy_late, h_all = lax.optimization_barrier((gy, h_all))
+        gy_late, stats_rows = lax.optimization_barrier((gy, stats_rows))
         gy_all = lax.all_gather(gy_late, 'sp', axis=0, tiled=True)
+        q, k, v, hat_q, hat_k = qkv_heads(h_all, w_pad, stats_rows, gains, n_dev, n_batch, tok, seq)
         o, d_q, d_k, d_v = attention(q, k, v, d_o, slopes, head_dim, math.gcd(seq, 512))
 
-        rstd = stats.reshape(n_dev, 4, n_batch, tok).transpose(1, 2, 0, 3).reshape(4, n_batch, seq)
+        def gathered(a):
+            return lax.all_gather(a, 'sp', axis=0, tiled=True)
+
+        dw_v = head_grads(d_v, h_all, n_dev, n_batch, tok, head_dim)
+        dw_v, d_q, d_k = lax.optimization_barrier((dw_v, d_q, d_k))
+        dw_v = gathered(dw_v)
+
         dq32, dk32 = d_q.astype(F32), d_k.astype(F32)
         gq = dq32 * gain_q[None, :, None, :]
         gk = dk32 * gain_k[None, :, None, :]
         part = jnp.stack([jnp.sum(gq, (1, 3)), jnp.sum(gq * hat_q, (1, 3)), jnp.sum(gk, (1, 3)), jnp.sum(gk * hat_k, (1, 3))])
-        full = jnp.sum(exchange(part.reshape(-1, LANES), n_dev), axis=0).reshape(4, n_batch, seq) * (1.0 / d_model)
-
-        def norm_back(g, hat, c1, c2, r):
-            e = lambda a: a[:, None, :, None]
-            return (e(r) * (g - e(c1) - hat * e(c2))).astype(BF16)
-
-        dq_raw = norm_back(gq, hat_q, full[0], full[1], rstd[1])
-        dk_raw = norm_back(gk, hat_k, full[2], full[3], rstd[3])
+        part = part.reshape(4 * n_batch, n_dev, tok).transpose(1, 0, 2)
+        part = exchange(part, n_dev, scatter=True)
+        own = jnp.sum(part, axis=0) * (1.0 / d_model)
+        full = exchange(own, n_dev).reshape(n_dev, 4, n_batch, tok).transpose(0, 2, 3, 1).reshape(n_dev * rows, 4)
+        cols = jnp.concatenate([stats_rows[:, 1:2], full[:, :2], stats_rows[:, 3:4], full[:, 2:]], axis=1)
         grad_q_ln = jnp.sum(dq32 * hat_q, (0, 2))[:, :head_dim]
         grad_k_ln = jnp.sum(dk32 * hat_k, (0, 2))[:, :head_dim]
 
-        def to_rows(a):
-            a = a[..., :head_dim].reshape(n_batch, n_h, n_dev, tok, head_dim)
-            return a.transpose(2, 0, 3, 1, 4).reshape(n_dev, rows, width)
-
-        back = jnp.concatenate([to_rows(a) for a in (dq_raw, dk_raw, d_v, o)], axis=-1)
-        back_flat = back.reshape(n_dev * rows, 4 * width)
+        dw_qk, back = norm_back(d_q, d_k, hat_q, hat_k, d_v, o, cols, gains, h_all, n_dev, n_batch, tok, head_dim)
+        o_late, dw_qk = lax.optimization_barrier((o, dw_qk))
+        dw_qk = gathered(dw_qk)
         tok_side = lax.all_to_all(back, 'sp', 0, 0, tiled=True)
-        dw_out = lax.dot_general(back_flat[:, 3 * width:], gy_all, (((0,), (0,)), ((), ())), preferred_element_type=F32)
-        dw_qkv_t = lax.dot_general(back_flat[:, :3 * width], h_all, (((0,), (0,)), ((), ())), preferred_element_type=F32)
-        grad_w_out = lax.all_gather(dw_out, 'sp', axis=0, tiled=True)
-        dw_all = lax.all_gather(dw_qkv_t, 'sp', axis=0, tiled=True)
-        grad_w_qkv = place_columns(dw_all.reshape(n_dev, 3, width, d_model), 4)
+        grad_w_out = gathered(head_grads(o_late, gy_all, n_dev, n_batch, tok, head_dim))
+        grad_w_qkv = place_columns(None, dw_v.reshape(n_dev, 1, width, d_model), 2, 3, 4)
+        grad_w_qkv = place_columns(grad_w_qkv, dw_qk.reshape(n_dev, 2, width, d_model), 0, 3, 4)
 
         o_tok = tok_side[:, :, 3 * width:].transpose(1, 0, 2).reshape(rows, d_model)
         y = (jnp.dot(o_tok, w_out, preferred_element_type=F32) + x_flat).astype(BF16)

time: 1130 us -> 1100 us (0.973)
  waiting for transfers between devices: 410 us -> 480 us
  local copies, waits for them, and re-layouts: 160 us -> 108 us
  matrix products: 118 us -> 72.2 us
  Pallas kernels: 329 us -> 358 us
  other arithmetic: 77.5 us -> 51.4 us
    all_gather x2 -> x3, waiting for transfers between devices: 55.6 us -> 221 us  [gathered(): return lax.all_gather(a, 'sp', axis=0, tiled=True)]
    all_gather x1, waiting for transfers between devices: 161 us -> 68.5 us  [local_step(): h_all = lax.all_gather(h_loc, 'sp', axis=0, tiled=True)]
    pallas_call x3 -> x7, Pallas kernels: 80.4 us -> 157 us  [the longest x2 64.7 us: head_grads(): pl.pallas_call(kernel, grid=(n_dev,), out_shape=jax.ShapeDtypeStruct((n_h...]
    pallas_call x1, Pallas kernels: 126 us -> 75.8 us  [attention(): pl.pallas_call(kernel, grid=(n_batch, n_h), out_shape=[jax.ShapeDtypeStru...]
    dot_general x2 -> x0, matrix products: 46.3 us -> none  [the longest x1 27.8 us: local_step(): lax.dot_general(back_flat[:, :3 * width], h_all, (((0,), (0,)), ((), ()))...]
    reshape x10 -> x3, local copies, waits for them, and re-layouts: 43.5 us -> 4.26 us  [the longest x1 3.5 us: local_step(): exchange(own, n_dev).reshape(n_dev, 4, n_batch, tok).transpose(0, 2, 3, 1)]
    all_to_all x1, waiting for transfers between devices: 193 us -> 159 us  [local_step(): tok_side = lax.all_to_all(back, 'sp', 0, 0, tiled=True)]
    all_to_all x1, waiting for transfers between devices: 0.01 us -> 30.3 us  [local_step(): d_o = lax.all_to_all(d_o, 'sp', 0, 0, tiled=True)]
  transfers between devices with their start and end apart: 6 -> 7, of which waited for: 3 -> 5; matrix products, arithmetic and copies ran while one was open for 27% -> 18% of each run, Pallas kernels for 22% -> 25%
where the time goes in v2:
time: 1100 us; the launch traced here: 1090 us
  waiting for transfers between devices  480 us (44%)
  Pallas kernels  358 us (33%)
  local copies, waits for them, and re-layouts  108 us (10%)
  matrix products  72.2 us (7%)
  other arithmetic  51.4 us (5%)
  between operations  14.5 us (1%)
    all_gather x3, waiting for transfers between devices, gathered(): return lax.all_gather(a, 'sp', axis=0, tiled=True)  221 us
    all_to_all x1, waiting for transfers between devices, local_step(): tok_side = lax.all_to_all(back, 'sp', 0, 0, tiled=True)  159 us
    pallas_call x2, Pallas kernels, place_columns(): pl.pallas_call(kernel, grid=(parts, n_grp, d_in // mb), out_shape=jax.Sha...  82.2 us
    pallas_call x1, Pallas kernels, attention(): pl.pallas_call(kernel, grid=(n_batch, n_h), out_shape=[jax.ShapeDtypeStru...  75.8 us
    all_gather x1, waiting for transfers between devices, local_step(): h_all = lax.all_gather(h_loc, 'sp', axis=0, tiled=True)  68.5 us
    pallas_call x2, Pallas kernels, head_grads(): pl.pallas_call(kernel, grid=(n_dev,), out_shape=jax.ShapeDtypeStruct((n_h...  64.7 us
    pallas_call x1, Pallas kernels, norm_back(): pl.pallas_call(kernel, grid=(n_dev,), out_shape=[jax.ShapeDtypeStruct((2...  51.8 us
    pallas_call x1, Pallas kernels, qkv_heads(): pl.pallas_call(kernel, grid=(n_dev,), out_shape=[jax.ShapeDtypeStruct(sha...  42.5 us
  transfers between devices with their start and end apart: 7, of which 5 were waited for; matrix products, arithmetic and copies ran while one was open for 18% of the time, Pallas kernels for 25%

profile of v2, /device:TPU:1, one launch (start us, length us, event | category | flops | bytes accessed | tf_op | source)
XLA Modules:
  0.0 1091.6 jit_solution(735985580236818520)
XLA Ops:
  16.4 21.8 %fusion = f32[512,5120]{1,0:T(8,128)} fusion(bf16[512,2560]{1,0:T(8,128)(2,1)} %fusion.17, bf16[2560,7680]{1,0:T(8,128)(2,1)} %param.9), kind=kOutput, calls=%fused_computation | convolution fusion | flops 13421772800 | bytes 39321600 | tf_op jit(solution)/shard_map/dot_general | solution.py:303
  47.3 11.2 %exchange.3 = f32[16,4,512]{2,1,0:T(4,128)} custom-call(f32[4,512]{1,0:T(4,128)} %pad_maximum_fusion.2.x_ref), custom_call_target="tpu_custom_call" | custom-call | tf_op jit(solution)/shard_map/exchange/pallas_call | solution.py:57
  62.1 11.1 %convert_bitcast_fusion = bf16[16,512,160]{1,2,0:T(8,128)(2,1)} fusion(bf16[16,160,2560]{2,1,0:T(8,128)(2,1)} %bitcast.115, bf16[512,2560,1]{1,0,2:T(8,128)(2,1)S(1)} %bitcast.95), kind=kOutput, calls=%fused_computation.41 | convolution fusion | flops 6712197120 | bytes 18350080 | tf_op jit(solution)/shard_map/te,nde->ntd/dot_general | solution.py:306
  94.2 30.3 %all-to-all-done = bf16[16,512,160]{1,2,0:T(8,128)(2,1)S(1)} async-done(((bf16[16,512,160]{1,2,0:T(8,128)(2,1)}), bf16[16,512,160]{1,2,0:T(8,128)(2,1)S(1)}, u32[]{:S(2)}, u32[]{:S(2)}) %all-to-all-start) | async-done | bytes 2621472 | tf_op jit(solution)/shard_map/all_to_all | solution.py:307
  139.8 68.5 %all-gather.6.cloned.1.call-done.h_ref.a_ref = bf16[8192,2560]{1,0:T(8,128)(2,1)} async-done(((bf16[512,2560]{1,0:T(8,128)(2,1)}), bf16[8192,2560]{1,0:T(8,128)(2,1)}) %all-gather.6.cloned.1.call-update) | async-done | bytes 41943056 | tf_op jit(solution)/shard_map/all_gather | solution.py:301
  208.3 42.5 %qkv_heads.1 = (bf16[4,2,2048,128]{3,2,1,0:T(8,128)(2,1)}, bf16[4,2,2048,128]{3,2,1,0:T(8,128)(2,1)}, bf16[4,2,2048,128]{3,2,1,0:T(8,128)(2,1)}, f32[4,2,2048,128]{3,2,1,0:T(8,128)}, f32[4,2,2048,128]{3,2,1,0:T(8,128)}) custom-call(bf16[8192,2560]{1,0:T(8,128)(2,1)} %all-gather.6.cloned.1.call-done.h_ref.a_ref, bf16[2560,768]{1,0:T(8,128)(2,1)} %copy-done.13, ...), custom_call_target="tpu_custom_call" | custom-call | flops 32212254720 | bytes 83886080 | tf_op jit(solution)/shard_map/qkv_heads/pallas_call | solution.py:89
  250.8 75.8 %attention.1 = (bf16[4,2,2048,128]{3,2,1,0:T(8,128)(2,1)}, bf16[4,2,2048,128]{3,2,1,0:T(8,128)(2,1)}, bf16[4,2,2048,128]{3,2,1,0:T(8,128)(2,1)}, bf16[4,2,2048,128]{3,2,1,0:T(8,128)(2,1)}) custom-call(f32[2]{0:T(128)} %dynamic_slice.18.slope_ref, bf16[4,2,2048,128]{3,2,1,0:T(8,128)(2,1)} %get-tuple-element.26.q_ref, ...), custom_call_target="tpu_custom_call" | custom-call | flops 51539607552 | bytes 41943040 | tf_op jit(solution)/shard_map/attention/pallas_call | solution.py:163
  326.6 37.9 %head_grads.2 = f32[160,2560]{1,0:T(8,128)} custom-call(bf16[4,2,2048,128]{3,2,1,0:T(8,128)(2,1)} %get-tuple-element.29.s_ref.dv_ref, bf16[8192,2560]{1,0:T(8,128)(2,1)} %all-gather.6.cloned.1.call-done.h_ref.a_ref), custom_call_target="tpu_custom_call" | custom-call | flops 10737418240 | bytes 52428800 | tf_op jit(solution)/shard_map/head_grads/pallas_call | solution.py:221
  364.5 8.4 fusion.9
  379.1 9.1 scatter_rows.1
  389.7 7.5 exchange.4
  415.0 51.8 %norm_back.1 = (f32[320,2560]{1,0:T(8,128)}, bf16[16,512,640]{2,1,0:T(8,128)(2,1)}) custom-call(bf16[4,2,2048,128]{3,2,1,0:T(8,128)(2,1)} %get-tuple-element.32.dq_ref, bf16[4,2,2048,128]{3,2,1,0:T(8,128)(2,1)} %get-tuple-element.33.dk_ref, f32[4,2,2048,128]{3,2,1,0:T(8,128)} %get-tuple-element.34.xq_ref, f32[4,2,2048,128]{3,2,1,0:T(8,128)} %get-tuple-element.35.xk_ref, ...), custom_call_target="tpu_custom_call" | custom-call | flops 21474836480 | bytes 94371840 | tf_op jit(solution)/shard_map/norm_back/pallas_call | solution.py:265
  466.8 26.8 %head_grads.3 = f32[160,2560]{1,0:T(8,128)} custom-call(bf16[4,2,2048,128]{3,2,1,0:T(8,128)(2,1)} %get-tuple-element.41.o_ref.s_ref, bf16[8192,2560]{1,0:T(8,128)(2,1)} %all-gather.12.cloned.1.call-done.a_ref), custom_call_target="tpu_custom_call" | custom-call | flops 10737418240 | bytes 52428800 | tf_op jit(solution)/shard_map/head_grads/pallas_call | solution.py:221
  499.0 159.2 %all-to-all-done.1 = bf16[16,512,640]{2,1,0:T(8,128)(2,1)} async-done(((bf16[16,512,640]{2,1,0:T(8,128)(2,1)}), bf16[16,512,640]{2,1,0:T(8,128)(2,1)}, u32[]{:S(2)}, u32[]{:S(2)}) %all-to-all-start.1) | async-done | bytes 10485792 | tf_op jit(solution)/shard_map/all_to_all | solution.py:344
  670.7 7.6 slice.88
  678.3 12.1 %copy.40 = bf16[16,512,480]{1,2,0:T(8,128)(2,1)} copy(bf16[16,512,480]{2,1,0:T(8,128)(2,1)} %slice.88) | data formatting | bytes 15728640 | tf_op jit(solution)/shard_map/slice | solution.py:351
  697.9 28.0 %fusion.12 = (f32[512]{0:T(512)S(1)}, bf16[512,2560]{1,0:T(8,128)(2,1)S(1)}) fusion(bf16[4,128,2560]{2,1,0:T(8,128)(2,1)S(1)} %copy-done.1, f32[2560]{0:T(1024)S(1)} %copy-done.12, f32[512]{0:T(512)S(1)} %copy-done.15, bf16[512,7680]{0,1:T(8,128)(2,1)} %bitcast.96, bf16[2560,7680]{1,0:T(8,128)(2,1)} %param.9), kind=kOutput, calls=%fused_computation.19 | convolution fusion | flops 20141834240 | bytes 52443136 | tf_op jit(solution)/shard_map/dot_general | solution.py:352
  730.7 13.0 %exchange.5 = f32[16,24,128]{2,1,0:T(8,128)} custom-call(f32[24,128]{1,0:T(8,128)} %pad_bitcast_fusion.x_ref), custom_call_target="tpu_custom_call" | custom-call | tf_op jit(solution)/shard_map/exchange/pallas_call | solution.py:57
  752.3 11.3 %fusion.20 = bf16[512,2560]{1,0:T(8,128)(2,1)} fusion(bf16[4,128,2560]{2,1,0:T(8,128)(2,1)S(1)} %copy-done.1, bf16[512,2560]{0,1:T(8,128)(2,1)S(1)} %bitcast.97, bf16[2560,2560]{1,0:T(8,128)(2,1)} %param.12), kind=kOutput, calls=%fused_computation.31 | convolution fusion | flops 6714818560 | bytes 20971520 | tf_op jit(solution)/shard_map/dot_general | solution.py:350
  763.6 53.8 %all-gather.10.cloned.1.call-done = f32[2560,2560]{1,0:T(8,128)} async-done(((f32[160,2560]{1,0:T(8,128)}), f32[2560,2560]{1,0:T(8,128)}) %all-gather.10.cloned.1.call-update) | async-done | bytes 26214416 | tf_op jit(solution)/shard_map/all_gather | solution.py:323
  817.5 27.8 %place_columns.2.refs_0_ = f32[2560,7680]{1,0:T(8,128)} custom-call(f32[16,1,160,2560]{3,2,1,0:T(8,128)} %bitcast.92), custom_call_target="tpu_custom_call" | custom-call | flops 13107200 | bytes 52428800 | tf_op jit(solution)/shard_map/place_columns/pallas_call | solution.py:186
  845.3 167.3 %all-gather.8.cloned.1.call-done = f32[5120,2560]{1,0:T(8,128)} async-done(((f32[320,2560]{1,0:T(8,128)}), f32[5120,2560]{1,0:T(8,128)}) %all-gather.8.cloned.1.call-update) | async-done | bytes 52428816 | tf_op jit(solution)/shard_map/all_gather | solution.py:323
  1012.6 54.4 %place_columns.3 = f32[2560,7680]{1,0:T(8,128)} custom-call(f32[16,2,160,2560]{3,2,1,0:T(8,128)} %bitcast.87, f32[2560,7680]{1,0:T(8,128)} %place_columns.2.refs_0_), custom_call_target="tpu_custom_call", output_to_operand_aliasing={{}: (1, {})} | custom-call | flops 26214400 | bytes 104857600 | tf_op jit(solution)/shard_map/place_columns/pallas_call | solution.py:186
  1067.0 17.5 %copy.54 = f32[2560,2560]{1,0:T(8,128)} copy(f32[2560,2560]{1,0:T(8,128)} %all-gather.14.cloned.1.call-done) | data formatting | bytes 52428800
  (111 shorter events, 122.1 us)
Async XLA Ops:
  7.2 6.8 copy-start
  7.2 201.1 %all-gather.6.cloned.1.call-start = ((), (), s32[]{:S(2)}) async-start(), calls=%async_computation.2 | async-start | bytes 44564480 | tf_op jit(solution)/shard_map/all_gather | solution.py:301
  8.1 5.3 copy-start.11
  10.2 3.2 copy-start.14
  16.4 450.4 %all-gather.12.cloned.1.call-start = ((), (), s32[]{:S(2)}) async-start(), calls=%async_computation.5 | async-start | bytes 44564480 | tf_op jit(solution)/shard_map/all_gather | solution.py:318
  38.2 7.0 copy-start.2
  46.6 15.4 %copy-start.9 = (bf16[4,128,2560]{2,1,0:T(8,128)(2,1)S(1)}, bf16[4,128,2560]{2,1,0:T(8,128)(2,1)}, u32[]{:S(2)}) copy-start(bf16[4,128,2560]{2,1,0:T(8,128)(2,1)} %param.13) | copy-start | bytes 7864324
  73.2 7.9 copy-start.20
  73.2 51.3 %all-to-all-start = ((bf16[16,512,160]{1,2,0:T(8,128)(2,1)}), bf16[16,512,160]{1,2,0:T(8,128)(2,1)S(1)}, u32[]{:S(2)}, u32[]{:S(2)}) async-start(bf16[16,512,160]{1,2,0:T(8,128)(2,1)} %convert_bitcast_fusion), calls=%async_computation | async-start | bytes 5242880 | tf_op jit(solution)/shard_map/all_to_all | solution.py:307
  75.9 687.7 %all-gather.14.cloned.1.call-start = ((), (), s32[]{:S(2)}) async-start(), calls=%async_computation.6 | async-start | bytes 27852800 | tf_op jit(solution)/shard_map/all_gather | solution.py:323
  78.1 10.6 copy-start.3
  364.5 8.4 copy-start.4
  364.5 8.9 copy-start.5
  400.7 6.8 copy-start.6
  400.7 6.8 copy-start.7
  493.6 323.8 %all-gather.10.cloned.1.call-start = ((), (), s32[]{:S(2)}) async-start(), calls=%async_computation.4 | async-start | bytes 27852800 | tf_op jit(solution)/shard_map/all_gather | solution.py:323
  494.2 518.4 %all-gather.8.cloned.1.call-start = ((), (), s32[]{:S(2)}) async-start(), calls=%async_computation.3 | async-start | bytes 55705600 | tf_op jit(solution)/shard_map/all_gather | solution.py:323
  494.8 163.4 %all-to-all-start.1 = ((bf16[16,512,640]{2,1,0:T(8,128)(2,1)}), bf16[16,512,640]{2,1,0:T(8,128)(2,1)}, u32[]{:S(2)}, u32[]{:S(2)}) async-start(bf16[16,512,640]{2,1,0:T(8,128)(2,1)} %get-tuple-element.37), calls=%async_computation.1 | async-start | bytes 20971520 | tf_op jit(solution)/shard_map/all_to_all | solution.py:344
  690.4 7.5 copy-start.1
  690.4 7.5 copy-start.12
  690.4 7.5 copy-start.15
  697.9 28.0 %copy-start.19 = (f32[4,128]{1,0:T(4,128)S(1)}, f32[4,128]{1,0:T(4,128)}, u32[]{:S(2)}) copy-start(f32[4,128]{1,0:T(4,128)} %copy-done.18) | copy-start | bytes 6148
  697.9 29.5 %copy-start.17 = (f32[512]{0:T(512)S(1)}, f32[512]{0:T(512)}, u32[]{:S(2)}) copy-start(f32[512]{0:T(512)} %copy-done.16) | copy-start | bytes 6148
  746.7 5.6 copy-start.10
  (4 other events, 4.5 us)
Sparse Core Ops, SparseCore 0:
  16.5 191.7 all-gather.5
  210.5 158.7 all-gather.11
  493.7 210.4 all-gather.13
  706.4 111.0 all-gather.9
  819.5 193.0 all-gather.7

commit v3 on v2

--- a/solution.py
+++ b/solution.py
@@ -65,6 +65,46 @@
     )(block)
 
 
+def norm_rows(x, weight, blk):
+    rows, d_model = x.shape
+
+    def kernel(x_ref, w_ref, o_ref):
+        o_ref[...] = layer_norm(x_ref[...].astype(F32), w_ref[...]).astype(BF16)
+
+    return pl.pallas_call(
+        kernel,
+        grid=(rows // blk,),
+        out_shape=jax.ShapeDtypeStruct(x.shape, BF16),
+        in_specs=[pl.BlockSpec((blk, d_model), lambda i: (i, 0)), pl.BlockSpec((1, d_model), lambda i: (0, 0))],
+        out_specs=pl.BlockSpec((blk, d_model), lambda i: (i, 0)),
+        cost_estimate=pl.CostEstimate(flops=8 * rows * d_model, bytes_accessed=4 * rows * d_model, transcendentals=0),
+        name='norm_rows',
+    )(x, weight)
+
+
+def columns_of(weight, rows_in, blk):
+    n_out, d_in = weight.shape
+    rows = rows_in.shape[0]
+
+    def kernel(w_ref, r_ref, o_ref):
+        o_ref[...] = lax.dot_general(w_ref[...], r_ref[...], (((1,), (1,)), ((), ())), preferred_element_type=F32).astype(BF16)
+
+    return pl.pallas_call(
+        kernel,
+        grid=(n_out // blk,),
+        out_shape=jax.ShapeDtypeStruct((n_out, rows), BF16),
+        in_specs=[pl.BlockSpec((blk, d_in), lambda i: (i, 0)), pl.BlockSpec((rows, d_in), lambda i: (0, 0))],
+        out_specs=pl.BlockSpec((blk, rows), lambda i: (i, 0)),
+        compiler_params=pltpu.CompilerParams(vmem_limit_bytes=40 * 2 ** 20),
+        cost_estimate=pl.CostEstimate(flops=2 * n_out * d_in * rows, bytes_accessed=2 * (n_out + rows) * d_in, transcendentals=0),
+        name='columns_of',
+    )(weight, rows_in)
+
+
+def token_cols(block, n_batch):
+    return jnp.concatenate([block[8 * b:8 * b + 8, :].T for b in range(n_batch)], axis=0)
+
+
 def qkv_heads(h_all, w_pad, stats, gains, n_dev, n_batch, tok, seq):
     rows = n_batch * tok
     d_model = h_all.shape[-1]
@@ -72,7 +112,7 @@
 
     def kernel(h_ref, w_ref, st_ref, g_ref, q_ref, k_ref, v_ref, xq_ref, xk_ref):
         raw = jnp.dot(h_ref[...], w_ref[...], preferred_element_type=F32)
-        st = st_ref[...]
+        st = token_cols(st_ref[0], n_batch)
         for n in range(n_h):
             for part, (o_ref, x_ref) in enumerate(((q_ref, xq_ref), (k_ref, xk_ref))):
                 col = (part * n_h + n) * LANES
@@ -91,7 +131,7 @@
         grid=(n_dev,),
         out_shape=[jax.ShapeDtypeStruct(shape, BF16)] * 3 + [jax.ShapeDtypeStruct(shape, F32)] * 2,
         in_specs=[pl.BlockSpec((rows, d_model), lambda i: (i, 0)), pl.BlockSpec((d_model, n_col), lambda i: (0, 0)),
-                  pl.BlockSpec((rows, stats.shape[1]), lambda i: (i, 0)), pl.BlockSpec(gains.shape, lambda i: (0, 0))],
+                  pl.BlockSpec((1,) + stats.shape[1:], lambda i: (i, 0, 0)), pl.BlockSpec(gains.shape, lambda i: (0, 0))],
         out_specs=[spec] * 5,
         compiler_params=pltpu.CompilerParams(vmem_limit_bytes=60 * 2 ** 20),
         cost_estimate=pl.CostEstimate(flops=2 * n_dev * rows * d_model * n_col, bytes_accessed=80 * 2 ** 20, transcendentals=0),
@@ -99,28 +139,50 @@
     )(h_all, w_pad, stats, gains)
 
 
-def attention(q, k, v, d_o, slopes, head_dim, blk):
+def attention(q, k, v, d_o, hat_q, hat_k, gains, slopes, head_dim, blk):
     n_batch, n_h, seq, _ = q.shape
     n_blk = seq // blk
+    tok = d_o.shape[-1] // n_batch
+    n_grp = blk // tok
     scale = head_dim ** -0.5
 
     def dot(a, b):
         return jnp.dot(a, b, preferred_element_type=F32)
 
-    def kernel(slope_ref, q_ref, k_ref, v_ref, do_ref, o_ref, dq_ref, dk_ref, dv_ref, w_ref, dk_acc, dv_acc, kt_ref, vt_ref):
+    def kernel(slope_ref, q_ref, k_ref, v_ref, do_ref, xq_ref, xk_ref, gq_ref, gk_ref, o_ref, dq_ref, dk_ref, dv_ref, sum_ref, gl_ref, w_ref, dk_acc, dv_acc, kt_ref, vt_ref):
         slope2 = slope_ref[pl.program_id(1)] * LOG2E
         dk_acc[...] = jnp.zeros_like(dk_acc)
         dv_acc[...] = jnp.zeros_like(dv_acc)
         kt_ref[...] = k_ref[0, 0].T
         vt_ref[...] = v_ref[0, 0].T
+        sum_ref[...] = jnp.zeros_like(sum_ref)
+        gl_ref[...] = jnp.zeros_like(gl_ref)
+
+        def norm_terms(part, rows, d_b, x_ref, g_ref):
+            gain = g_ref[0]
+            prod = d_b.astype(F32) * x_ref[0, 0, rows, :]
+            gl_ref[0, 0, part:part + 1, :] += jnp.sum(prod, axis=0, keepdims=True)
+            prod = prod * gain
+            pieces = [d_b]
+            for _ in range(3):
+                pieces.append(prod.astype(BF16))
+                prod = prod - pieces[-1].astype(F32)
+            row = lax.broadcasted_iota(jnp.int32, (8, LANES), 0)
+            first = jnp.where(row == 0, jnp.broadcast_to(gain, (8, LANES)), 0.0).astype(BF16)
+            other = jnp.where(row == 1, 1.0, 0.0).astype(BF16)
+            lhs = jnp.concatenate([first, other, other, other], axis=1)
+            both = lax.dot_general(lhs, jnp.concatenate(pieces, axis=1), (((1,), (1,)), ((), ())), preferred_element_type=F32)
+            sum_ref[0, 0, 2 * part:2 * part + 2, rows] = both[:2]
+
         key_iota = lax.broadcasted_iota(jnp.int32, (blk, LANES), 0)[:, :1]
         blocks = [pl.ds(j * blk, blk) for j in range(n_blk)]
 
         for i in range(n_blk):
             q_b = q_ref[0, 0, blocks[i], :]
-            do_b = do_ref[0, 0, blocks[i], :]
             q_t = q_b.T
-            do_t = do_b.T
+            do_t = jnp.concatenate([do_ref[i * n_grp + m, 0] for m in range(n_grp)], axis=1)
+            do_t = jnp.concatenate([do_t, jnp.zeros((LANES - head_dim, blk), BF16)], axis=0)
+            do_b = do_t.T
             top = None
             for j in range(i, -1, -1):
                 s = dot(k_ref[0, 0, blocks[j], :], q_t) * (scale * LOG2E)
@@ -153,9 +215,14 @@
                 d_s = (p * (d_p - delta)).astype(BF16)
                 dk_acc[blocks[j], :] += dot(d_s, q_b)
                 dq_t = dq_t + dot(kt_ref[:, blocks[j]], d_s)
-            dq_ref[0, 0, blocks[i], :] = (dq_t * scale).T.astype(BF16)
-
-        dk_ref[0, 0] = (dk_acc[...] * scale).astype(BF16)
+            dq_b = (dq_t * scale).T.astype(BF16)
+            dq_ref[0, 0, blocks[i], :] = dq_b
+            norm_terms(0, blocks[i], dq_b, xq_ref, gq_ref)
+
+        for j in range(n_blk):
+            dk_b = (dk_acc[blocks[j], :] * scale).astype(BF16)
+            dk_ref[0, 0, blocks[j], :] = dk_b
+            norm_terms(1, blocks[j], dk_b, xk_ref, gk_ref)
         dv_ref[0, 0] = dv_acc[...].astype(BF16)
 
     spec = pl.BlockSpec((1, 1, seq, LANES), lambda b, n: (b, n, 0, 0))
@@ -163,19 +230,20 @@
     return pl.pallas_call(
         kernel,
         grid=(n_batch, n_h),
-        out_shape=[jax.ShapeDtypeStruct(q.shape, BF16)] * 4,
-        in_specs=[pl.BlockSpec(memory_space=pltpu.SMEM)] + [spec] * 4,
-        out_specs=[spec] * 4,
+        out_shape=[jax.ShapeDtypeStruct(q.shape, BF16)] * 4 + [jax.ShapeDtypeStruct((n_batch, n_h, 8, n), F32) for n in (seq, LANES)],
+        in_specs=[pl.BlockSpec(memory_space=pltpu.SMEM)] + [spec] * 3 + [pl.BlockSpec((seq // tok, 1, head_dim, tok), lambda b, n: (0, n, 0, b))] + [spec] * 2 + [pl.BlockSpec((1, 1, LANES), lambda b, n: (n, 0, 0)), pl.BlockSpec((1, 1, LANES), lambda b, n: (n_h + n, 0, 0))],
+        out_specs=[spec] * 4 + [pl.BlockSpec((1, 1, 8, n), lambda b, n: (b, n, 0, 0)) for n in (seq, LANES)],
         scratch_shapes=[pltpu.VMEM((seq, blk), F32), pltpu.VMEM((seq, LANES), F32), pltpu.VMEM((seq, LANES), F32),
                         pltpu.VMEM((LANES, seq), BF16), pltpu.VMEM((LANES, seq), BF16)],
         compiler_params=pltpu.CompilerParams(vmem_limit_bytes=60 * 2 ** 20),
         cost_estimate=pl.CostEstimate(flops=flops, bytes_accessed=40 * 2 ** 20, transcendentals=n_batch * n_h * seq * seq // 2),
         name='attention',
-    )(slopes, q, k, v, d_o)
-
-
-def place_columns(buf, gathered, first, n_part, group):
-    n_dev, parts, width, d_in = gathered.shape
+    )(slopes, q, k, v, d_o, hat_q, hat_k, gains[:, None], gains[:, None])
+
+
+def place_columns(buf, gathered, first, n_part, group, parts=1):
+    n_dev, _, d_in = gathered.shape
+    width = d_in // n_dev
     mb = 512 if d_in % 512 == 0 else d_in
     n_grp = n_dev // group
 
@@ -187,13 +255,53 @@
         kernel,
         grid=(parts, n_grp, d_in // mb),
         out_shape=jax.ShapeDtypeStruct((d_in, n_part * n_dev * width), gathered.dtype),
-        in_specs=[pl.BlockSpec((group, 1, width, mb), lambda p, g, m: (g, p, 0, m))] + [pl.BlockSpec(memory_space=pl.ANY)] * (len(args) - 1),
+        in_specs=[pl.BlockSpec((group, width, mb), lambda p, g, m: (g, p, m))] + [pl.BlockSpec(memory_space=pl.ANY)] * (len(args) - 1),
         out_specs=pl.BlockSpec((mb, group * width), lambda p, g, m: (m, (p + first) * n_grp + g)),
         input_output_aliases={1: 0} if buf is not None else {},
         compiler_params=pltpu.CompilerParams(vmem_limit_bytes=40 * 2 ** 20),
-        cost_estimate=pl.CostEstimate(flops=2 * gathered.size, bytes_accessed=8 * gathered.size, transcendentals=0),
+        cost_estimate=pl.CostEstimate(flops=parts * d_in * d_in, bytes_accessed=8 * parts * d_in * d_in, transcendentals=0),
         name='place_columns',
     )(*args)
+
+
+def place_rows(buf, gathered, first, n_rows, half, n_half):
+    n_dev, _, d_in = gathered.shape
+    group = math.gcd(n_dev, 4)
+
+    def kernel(x_ref, *refs):
+        refs[-1][:, 0] = x_ref[...]
+
+    args = (gathered,) if buf is None else (gathered, buf)
+    return pl.pallas_call(
+        kernel,
+        grid=(n_dev // group,),
+        out_shape=jax.ShapeDtypeStruct((n_dev, n_half, n_rows, d_in), gathered.dtype),
+        in_specs=[pl.BlockSpec((group, n_rows, d_in), lambda i: (i, first // n_rows, 0))] + [pl.BlockSpec(memory_space=pl.ANY)] * (len(args) - 1),
+        out_specs=pl.BlockSpec((group, 1, n_rows, d_in), lambda i: (i, half, 0, 0)),
+        input_output_aliases={1: 0} if buf is not None else {},
+        compiler_params=pltpu.CompilerParams(vmem_limit_bytes=40 * 2 ** 20),
+        cost_estimate=pl.CostEstimate(flops=n_dev * n_rows * d_in, bytes_accessed=8 * n_dev * n_rows * d_in, transcendentals=0),
+        name='place_rows',
+    )(*args)
+
+
+def token_rows(arrays, n_dev, n_batch, tok, head_dim):
+    n_h = arrays[0].shape[1]
+    rows = n_batch * tok
+    width = len(arrays) * n_h * head_dim
+
+    def kernel(*refs):
+        refs[-1][0] = jnp.concatenate([ref[:, n].reshape(rows, LANES).T[:head_dim] for ref in refs[:-1] for n in range(n_h)], axis=0)
+
+    return pl.pallas_call(
+        kernel,
+        grid=(n_dev,),
+        out_shape=jax.ShapeDtypeStruct((n_dev, width, rows), BF16),
+        in_specs=[pl.BlockSpec((n_batch, n_h, tok, LANES), lambda i: (0, 0, i, 0))] * len(arrays),
+        out_specs=pl.BlockSpec((1, width, rows), lambda i: (i, 0, 0)),
+        cost_estimate=pl.CostEstimate(flops=n_dev * rows * width, bytes_accessed=4 * n_dev * rows * width, transcendentals=0),
+        name='token_rows',
+    )(*arrays)
 
 
 def head_grads(side, acts, n_dev, n_batch, tok, head_dim):
@@ -203,15 +311,12 @@
     def kernel(s_ref, a_ref, o_ref, acc):
         step = pl.program_id(0)
         lhs = jnp.concatenate([s_ref[:, n].reshape(rows, LANES) for n in range(n_h)], axis=1)
-        out = lax.dot_general(lhs, a_ref[...], (((0,), (0,)), ((), ())), preferred_element_type=F32)
 
         @pl.when(step == 0)
         def _():
-            acc[...] = out
-
-        @pl.when(step > 0)
-        def _():
-            acc[...] += out
+            acc[...] = jnp.zeros_like(acc)
+
+        acc[...] += lax.dot_general(lhs, a_ref[...], (((0,), (0,)), ((), ())), preferred_element_type=F32)
 
         @pl.when(step == n_dev - 1)
         def _():
@@ -231,30 +336,29 @@
     )(side, acts)
 
 
-def norm_back(d_q, d_k, hat_q, hat_k, d_v, o, cols, gains, acts, n_dev, n_batch, tok, head_dim):
+def norm_back(d_q, d_k, hat_q, hat_k, stats, sums, gains, acts, n_dev, n_batch, tok, head_dim):
     n_h = d_q.shape[1]
     rows, d_model = n_batch * tok, acts.shape[-1]
     width = n_h * head_dim
 
-    def kernel(dq_ref, dk_ref, xq_ref, xk_ref, dv_ref, o_ref, c_ref, g_ref, a_ref, w_ref, b_ref, acc):
+    def kernel(dq_ref, dk_ref, xq_ref, xk_ref, st_ref, c_ref, g_ref, a_ref, w_ref, b_ref, acc):
         step = pl.program_id(0)
+        st = token_cols(st_ref[0], n_batch)
+        cols = token_cols(c_ref[0], n_batch)
         sides = []
         for part, (d_ref, x_ref) in enumerate(((dq_ref, xq_ref), (dk_ref, xk_ref))):
-            r, c1, c2 = (c_ref[:, 3 * part + m:3 * part + m + 1] for m in range(3))
+            r = st[:, 2 * part + 1:2 * part + 2]
+            c1, c2 = (cols[:, 2 * part + m:2 * part + m + 1] for m in range(2))
             for n in range(n_h):
                 g = d_ref[:, n].reshape(rows, LANES).astype(F32) * g_ref[part * n_h + n:part * n_h + n + 1, :]
                 sides.append((r * (g - c1 - x_ref[:, n].reshape(rows, LANES) * c2)).astype(BF16))
-        out = lax.dot_general(jnp.concatenate(sides, axis=1), a_ref[...], (((0,), (0,)), ((), ())), preferred_element_type=F32)
-        sides += [ref[:, n].reshape(rows, LANES) for ref in (dv_ref, o_ref) for n in range(n_h)]
-        b_ref[0] = jnp.concatenate([a[:, :head_dim] for a in sides], axis=1)
+        b_ref[0] = jnp.concatenate([a.T[:head_dim] for a in sides], axis=0)
 
         @pl.when(step == 0)
         def _():
-            acc[...] = out
-
-        @pl.when(step > 0)
-        def _():
-            acc[...] += out
+            acc[...] = jnp.zeros_like(acc)
+
+        acc[...] += lax.dot_general(jnp.concatenate(sides, axis=1), a_ref[...], (((0,), (0,)), ((), ())), preferred_element_type=F32)
 
         @pl.when(step == n_dev - 1)
         def _():
@@ -265,15 +369,15 @@
     return pl.pallas_call(
         kernel,
         grid=(n_dev,),
-        out_shape=[jax.ShapeDtypeStruct((2 * width, d_model), F32), jax.ShapeDtypeStruct((n_dev, rows, 4 * width), BF16)],
-        in_specs=[heads] * 6 + [pl.BlockSpec((rows, cols.shape[1]), lambda i: (i, 0)), pl.BlockSpec(gains.shape, lambda i: (0, 0)),
+        out_shape=[jax.ShapeDtypeStruct((2 * width, d_model), F32), jax.ShapeDtypeStruct((n_dev, 2 * width, rows), BF16)],
+        in_specs=[heads] * 4 + [pl.BlockSpec((1,) + stats.shape[1:], lambda i: (i, 0, 0))] * 2 + [pl.BlockSpec(gains.shape, lambda i: (0, 0)),
                                 pl.BlockSpec((rows, d_model), lambda i: (i, 0))],
-        out_specs=[pl.BlockSpec((2 * width, d_model), lambda i: (0, 0)), pl.BlockSpec((1, rows, 4 * width), lambda i: (i, 0, 0))],
+        out_specs=[pl.BlockSpec((2 * width, d_model), lambda i: (0, 0)), pl.BlockSpec((1, 2 * width, rows), lambda i: (i, 0, 0))],
         scratch_shapes=[pltpu.VMEM((2 * n_h * LANES, d_model), F32)],
         compiler_params=pltpu.CompilerParams(vmem_limit_bytes=60 * 2 ** 20),
         cost_estimate=pl.CostEstimate(flops=4 * n_dev * rows * d_model * n_h * LANES, bytes_accessed=90 * 2 ** 20, transcendentals=0),
         name='norm_back',
-    )(d_q, d_k, hat_q, hat_k, d_v, o, cols, gains, acts)
+    )(d_q, d_k, hat_q, hat_k, stats, sums, gains, acts)
 
 
 def solution(mesh):
@@ -296,60 +400,62 @@
 
         x_flat = x.reshape(rows, d_model).astype(F32)
         gy = grad_y.reshape(rows, d_model)
-        h_f32, ln1_pull = jax.vjp(layer_norm, x_flat, ln1_w.astype(F32))
-        h_loc = h_f32.astype(BF16)
+        h_loc = norm_rows(x.reshape(rows, d_model), ln1_w.astype(F32).reshape(1, d_model), math.gcd(rows, 128))
         h_all = lax.all_gather(h_loc, 'sp', axis=0, tiled=True)
 
         qk_raw = jnp.dot(h_loc, w_qkv[:, :2 * d_model], preferred_element_type=F32)
-        stats_loc = jnp.stack(row_stats(qk_raw[:, :d_model]) + row_stats(qk_raw[:, d_model:]))
+        stats_loc = jnp.stack(row_stats(qk_raw[:, :d_model]) + row_stats(qk_raw[:, d_model:])).reshape(4, n_batch, tok)
+        stats_loc = jnp.pad(stats_loc.transpose(1, 0, 2), ((0, 0), (0, 4), (0, 0))).reshape(8 * n_batch, tok)
         stats = exchange(stats_loc, n_dev)
-        d_o = jnp.einsum('te,nde->ntd', gy, w_out.reshape(n_dev, width, d_model), preferred_element_type=F32).astype(BF16)
+        d_o = columns_of(w_out, gy, 4 * width).reshape(n_dev, width, rows)
+        d_o, h_all = lax.optimization_barrier((d_o, h_all))
         d_o = lax.all_to_all(d_o, 'sp', 0, 0, tiled=True)
-        d_o = d_o.reshape(n_dev, n_batch, tok, n_h, head_dim).transpose(1, 3, 0, 2, 4).reshape(n_batch, n_h, seq, head_dim)
-        d_o = pad_lanes(d_o)
+        d_o = d_o.reshape(n_dev, n_h, head_dim, rows)
         slices = [lax.dynamic_slice_in_dim(w_qkv, p * d_model + me * width, width, axis=1) for p in range(3)]
         w_pad = jnp.concatenate([pad_lanes(s[:, n * head_dim:(n + 1) * head_dim]) for s in slices for n in range(n_h)], axis=1)
         gain_q = pad_lanes(lax.dynamic_slice_in_dim(q_ln_w, me * n_h, n_h).astype(F32))
         gain_k = pad_lanes(lax.dynamic_slice_in_dim(k_ln_w, me * n_h, n_h).astype(F32))
         gains = jnp.concatenate([gain_q, gain_k])
-        stats_rows = stats.transpose(0, 2, 1).reshape(n_dev * rows, 4)
-
-        gy_late, stats_rows = lax.optimization_barrier((gy, stats_rows))
+
+        gy_late, stats = lax.optimization_barrier((gy, stats))
         gy_all = lax.all_gather(gy_late, 'sp', axis=0, tiled=True)
-        q, k, v, hat_q, hat_k = qkv_heads(h_all, w_pad, stats_rows, gains, n_dev, n_batch, tok, seq)
-        o, d_q, d_k, d_v = attention(q, k, v, d_o, slopes, head_dim, math.gcd(seq, 512))
+        q, k, v, hat_q, hat_k = qkv_heads(h_all, w_pad, stats, gains, n_dev, n_batch, tok, seq)
+        o, d_q, d_k, d_v, head_sums, head_ln = attention(q, k, v, d_o, hat_q, hat_k, gains, slopes, head_dim, math.gcd(seq, 512))
 
         def gathered(a):
             return lax.all_gather(a, 'sp', axis=0, tiled=True)
 
         dw_v = head_grads(d_v, h_all, n_dev, n_batch, tok, head_dim)
-        dw_v, d_q, d_k = lax.optimization_barrier((dw_v, d_q, d_k))
+        dw_v, d_q, d_k, head_sums = lax.optimization_barrier((dw_v, d_q, d_k, head_sums))
         dw_v = gathered(dw_v)
 
-        dq32, dk32 = d_q.astype(F32), d_k.astype(F32)
-        gq = dq32 * gain_q[None, :, None, :]
-        gk = dk32 * gain_k[None, :, None, :]
-        part = jnp.stack([jnp.sum(gq, (1, 3)), jnp.sum(gq * hat_q, (1, 3)), jnp.sum(gk, (1, 3)), jnp.sum(gk * hat_k, (1, 3))])
-        part = part.reshape(4 * n_batch, n_dev, tok).transpose(1, 0, 2)
+        part = jnp.sum(head_sums, axis=1).reshape(n_batch, 8, n_dev, tok).transpose(2, 0, 1, 3).reshape(n_dev, 8 * n_batch, tok)
+        grad_q_ln, grad_k_ln = jnp.sum(head_ln, axis=0)[:, :2, :head_dim].transpose(1, 0, 2)
         part = exchange(part, n_dev, scatter=True)
-        own = jnp.sum(part, axis=0) * (1.0 / d_model)
-        full = exchange(own, n_dev).reshape(n_dev, 4, n_batch, tok).transpose(0, 2, 3, 1).reshape(n_dev * rows, 4)
-        cols = jnp.concatenate([stats_rows[:, 1:2], full[:, :2], stats_rows[:, 3:4], full[:, 2:]], axis=1)
-        grad_q_ln = jnp.sum(dq32 * hat_q, (0, 2))[:, :head_dim]
-        grad_k_ln = jnp.sum(dk32 * hat_k, (0, 2))[:, :head_dim]
-
-        dw_qk, back = norm_back(d_q, d_k, hat_q, hat_k, d_v, o, cols, gains, h_all, n_dev, n_batch, tok, head_dim)
+        sums = exchange(jnp.sum(part, axis=0) * (1.0 / d_model), n_dev)
+
+        d_v, o, sums = lax.optimization_barrier((d_v, o, sums))
+        tok_ov = lax.all_to_all(token_rows((d_v, o), n_dev, n_batch, tok, head_dim), 'sp', 0, 0, tiled=True)
+        dw_qk, back_qk = norm_back(d_q, d_k, hat_q, hat_k, stats, sums, gains, h_all, n_dev, n_batch, tok, head_dim)
+        tok_qk = lax.all_to_all(back_qk, 'sp', 0, 0, tiled=True)
         o_late, dw_qk = lax.optimization_barrier((o, dw_qk))
-        dw_qk = gathered(dw_qk)
-        tok_side = lax.all_to_all(back, 'sp', 0, 0, tiled=True)
-        grad_w_out = gathered(head_grads(o_late, gy_all, n_dev, n_batch, tok, head_dim))
-        grad_w_qkv = place_columns(None, dw_v.reshape(n_dev, 1, width, d_model), 2, 3, 4)
-        grad_w_qkv = place_columns(grad_w_qkv, dw_qk.reshape(n_dev, 2, width, d_model), 0, 3, 4)
-
-        o_tok = tok_side[:, :, 3 * width:].transpose(1, 0, 2).reshape(rows, d_model)
-        y = (jnp.dot(o_tok, w_out, preferred_element_type=F32) + x_flat).astype(BF16)
-        d_qkv = tok_side[:, :, :3 * width].reshape(n_dev, rows, 3, width).transpose(1, 2, 0, 3).reshape(rows, 3 * d_model)
-        d_h = lax.dot_general(d_qkv, w_qkv, (((1,), (1,)), ((), ())), preferred_element_type=F32).astype(BF16)
+        dw_out = head_grads(o_late, gy_all, n_dev, n_batch, tok, head_dim)
+        half = width // 2
+        dw_qko = gathered(jnp.concatenate([dw_qk, dw_out[:half]])).reshape(n_dev, 2 * width + half, d_model)
+        dw_last = gathered(dw_out[half:]).reshape(n_dev, half, d_model)
+        grad_w_qkv = place_columns(None, dw_v.reshape(n_dev, width, d_model), 2, 3, 4)
+        grad_w_qkv = place_columns(grad_w_qkv, dw_qko, 0, 3, 4, parts=2)
+        grad_w_out = place_rows(None, dw_qko, 2 * width, half, 0, 2)
+        grad_w_out = place_rows(grad_w_out, dw_last, 0, half, 1, 2).reshape(d_model, d_model)
+
+        def over_rows(cols, weight, w_dim):
+            return lax.dot_general(cols, weight, (((0,), (w_dim,)), ((), ())), preferred_element_type=F32)
+
+        o_cols = tok_ov[:, width:].reshape(d_model, rows)
+        y = (over_rows(o_cols, w_out, 0) + x_flat).astype(BF16)
+        d_cols = jnp.stack([tok_qk[:, :width], tok_qk[:, width:], tok_ov[:, :width]]).reshape(3 * d_model, rows)
+        d_h = over_rows(d_cols, w_qkv, 1).astype(BF16)
+        _, ln1_pull = jax.vjp(layer_norm, x_flat, ln1_w.astype(F32))
         d_x_norm, grad_ln1 = ln1_pull(d_h.astype(F32))
         grad_x = (d_x_norm + gy.astype(F32)).astype(BF16)
 

time: 1100 us -> 899 us (0.82)
  waiting for transfers between devices: 480 us -> 238 us
  blocking collectives: 0 us -> 94.8 us
  local copies, waits for them, and re-layouts: 108 us -> 35 us
  Pallas kernels: 358 us -> 395 us
  other arithmetic: 51.4 us -> 37.8 us
    all_gather x3, waiting for transfers between devices: 221 us -> 30.7 us  [gathered(): return lax.all_gather(a, 'sp', axis=0, tiled=True)]
    all_to_all x0 -> x1, blocking collectives: none -> 94.8 us  [local_step(): lax.all_to_all(token_rows((d_v, o), n_dev, n_batch, tok, head_dim), 'sp',...]
    all_to_all x1, waiting for transfers between devices: 159 us -> 106 us  [local_step(): tok_qk = lax.all_to_all(back_qk, 'sp', 0, 0, tiled=True)]
    pallas_call x0 -> x5, Pallas kernels: none -> 41.5 us  [the longest x2 14.8 us: place_rows(): pl.pallas_call(kernel, grid=(n_dev // group,), out_shape=jax.ShapeDtypeSt...]
    slice x4 -> x1, local copies, waits for them, and re-layouts: 31.9 us -> 1.02 us  [local_step(): dw_last = gathered(dw_out[half:]).reshape(n_dev, half, d_model)]
    all_gather x1, waiting for transfers between devices: 68.5 us -> 92.4 us  [local_step(): h_all = lax.all_gather(h_loc, 'sp', axis=0, tiled=True)]
    transpose x4 -> x2, local copies, waits for them, and re-layouts: 23.5 us -> 0.79 us  [the longest x1 0.78 us: local_step(): jnp.sum(head_sums, axis=1).reshape(n_batch, 8, n_dev, tok)]
    all_to_all x1, waiting for transfers between devices: 30.3 us -> 8.96 us  [local_step(): d_o = lax.all_to_all(d_o, 'sp', 0, 0, tiled=True)]
  transfers between devices with their start and end apart: 7 -> 7, of which waited for: 5 -> 5; matrix products, arithmetic and copies ran while one was open for 18% -> 14% of each run, Pallas kernels for 25% -> 43%
where the time goes in v3:
time: 899 us; the launch traced here: 888 us
  Pallas kernels  395 us (44%)
  waiting for transfers between devices  238 us (26%)
  blocking collectives  94.8 us (11%)
  matrix products  65.2 us (7%)
  other arithmetic  37.8 us (4%)
  local copies, waits for them, and re-layouts  35 us (4%)
  between operations  14.3 us (2%)
    all_to_all x1, waiting for transfers between devices, local_step(): tok_qk = lax.all_to_all(back_qk, 'sp', 0, 0, tiled=True)  106 us
    all_to_all x1, blocking collectives, local_step(): lax.all_to_all(token_rows((d_v, o), n_dev, n_batch, tok, head_dim), 'sp',...  94.8 us
    all_gather x1, waiting for transfers between devices, local_step(): h_all = lax.all_gather(h_loc, 'sp', axis=0, tiled=True)  92.4 us
    pallas_call x1, Pallas kernels, attention(): pl.pallas_call(kernel, grid=(n_batch, n_h), out_shape=[jax.ShapeDtypeStru...  90.9 us
    pallas_call x2, Pallas kernels, place_columns(): pl.pallas_call(kernel, grid=(parts, n_grp, d_in // mb), out_shape=jax.Sha...  82.1 us
    pallas_call x2, Pallas kernels, head_grads(): pl.pallas_call(kernel, grid=(n_dev,), out_shape=jax.ShapeDtypeStruct((n_h...  50.6 us
    pallas_call x1, Pallas kernels, norm_back(): pl.pallas_call(kernel, grid=(n_dev,), out_shape=[jax.ShapeDtypeStruct((2...  45.8 us
    dot_general x2, matrix products, over_rows(): lax.dot_general(cols, weight, (((0,), (w_dim,)), ((), ())), preferred_ele...  43.5 us
  transfers between devices with their start and end apart: 7, of which 5 were waited for; matrix products, arithmetic and copies ran while one was open for 14% of the time, Pallas kernels for 43%

profile of v3, /device:TPU:1, one launch (start us, length us, event | category | flops | bytes accessed | tf_op | source)
XLA Modules:
  0.0 887.7 jit_solution(12285748321896904380)
XLA Ops:
  13.4 21.8 %fusion = f32[512,5120]{1,0:T(8,128)} fusion(bf16[512,2560]{1,0:T(8,128)(2,1)} %norm_rows.1, bf16[2560,7680]{1,0:T(8,128)(2,1)} %param.9), kind=kOutput, calls=%fused_computation | convolution fusion | flops 13421772800 | bytes 39321600 | tf_op jit(solution)/shard_map/dot_general | solution.py:406
  44.3 14.0 %exchange.3.st_ref = f32[16,32,128]{2,1,0:T(8,128)} custom-call(f32[32,128]{1,0:T(8,128)} %pad_bitcast_fusion.x_ref), custom_call_target="tpu_custom_call" | custom-call | tf_op jit(solution)/shard_map/exchange/pallas_call | solution.py:57
  74.0 9.5 %columns_of.1 = bf16[2560,512]{1,0:T(8,128)(2,1)S(1)} custom-call(bf16[2560,2560]{1,0:T(8,128)(2,1)} %w_ref.1, bf16[512,2560]{1,0:T(8,128)(2,1)S(1)} %bitcast.71), custom_call_target="tpu_custom_call" | custom-call | flops 6710886400 | bytes 15728640 | tf_op jit(solution)/shard_map/columns_of/pallas_call | solution.py:92
  85.0 92.4 %all-gather.6.cloned.1.call-done.h_ref.a_ref = bf16[8192,2560]{1,0:T(8,128)(2,1)} async-done(((bf16[512,2560]{1,0:T(8,128)(2,1)}), bf16[8192,2560]{1,0:T(8,128)(2,1)}) %all-gather.6.cloned.1.call-update) | async-done | bytes 41943056 | tf_op jit(solution)/shard_map/all_gather | solution.py:404
  181.1 41.7 %qkv_heads.1 = (bf16[4,2,2048,128]{3,2,1,0:T(8,128)(2,1)}, bf16[4,2,2048,128]{3,2,1,0:T(8,128)(2,1)}, bf16[4,2,2048,128]{3,2,1,0:T(8,128)(2,1)}, f32[4,2,2048,128]{3,2,1,0:T(8,128)}, f32[4,2,2048,128]{3,2,1,0:T(8,128)}) custom-call(bf16[8192,2560]{1,0:T(8,128)(2,1)} %all-gather.6.cloned.1.call-done.h_ref.a_ref, ...), custom_call_target="tpu_custom_call" | custom-call | flops 32212254720 | bytes 83886080 | tf_op jit(solution)/shard_map/qkv_heads/pallas_call | solution.py:129
  222.8 9.0 %all-to-all-done = bf16[16,160,512]{2,1,0:T(8,128)(2,1)} async-done(((bf16[16,160,512]{2,1,0:T(8,128)(2,1)}), bf16[16,160,512]{2,1,0:T(8,128)(2,1)}, u32[]{:S(2)}, u32[]{:S(2)}) %all-to-all-start) | async-done | bytes 2621472 | tf_op jit(solution)/shard_map/all_to_all | solution.py:412
  231.8 90.9 %attention.1 = (bf16[4,2,2048,128]{3,2,1,0:T(8,128)(2,1)}, bf16[4,2,2048,128]{3,2,1,0:T(8,128)(2,1)}, bf16[4,2,2048,128]{3,2,1,0:T(8,128)(2,1)}, bf16[4,2,2048,1...) custom-call(f32[2]{0:T(128)} %dynamic_slice.18.slope_ref, ...), custom_call_target="tpu_custom_call" | custom-call | flops 51539607552 | bytes 41943040 | tf_op jit(solution)/shard_map/attention/pallas_call | solution.py:230
  322.6 24.5 %head_grads.2 = f32[160,2560]{1,0:T(8,128)S(1)} custom-call(bf16[4,2,2048,128]{3,2,1,0:T(8,128)(2,1)} %get-tuple-element.47.s_ref.refs_0_, bf16[8192,2560]{1,0:T(8,128)(2,1)} %all-gather.6.cloned.1.call-done.h_ref.a_ref), custom_call_target="tpu_custom_call" | custom-call | flops 10737418240 | bytes 52428800 | tf_op jit(solution)/shard_map/head_grads/pallas_call | solution.py:326
  349.3 9.9 %scatter_rows.1 = f32[16,32,128]{2,1,0:T(8,128)} custom-call(f32[16,32,128]{2,1,0:T(8,128)} %bitcast.83), custom_call_target="tpu_custom_call" | custom-call | tf_op jit(solution)/shard_map/scatter_rows/pallas_call | solution.py:57
  360.8 9.4 %exchange.4.c_ref = f32[16,32,128]{2,1,0:T(8,128)} custom-call(f32[32,128]{1,0:T(8,128)} %broadcast_multiply_fusion.x_ref), custom_call_target="tpu_custom_call" | custom-call | tf_op jit(solution)/shard_map/exchange/pallas_call | solution.py:57
  370.2 45.8 %norm_back.1 = (f32[320,2560]{1,0:T(8,128)}, bf16[16,320,512]{2,1,0:T(8,128)(2,1)}) custom-call(bf16[4,2,2048,128]{3,2,1,0:T(8,128)(2,1)} %get-tuple-element.49.dq_ref, bf16[4,2,2048,128]{3,2,1,0:T(8,128)(2,1)} %get-tuple-element.50.dk_ref, f32[4,2,2048,128]{3,2,1,0:T(8,128)} %get-tuple-element.39.xq_ref, f32[4,2,2048,128]{3,2,1,0:T(8,128)} %get-tuple-element.40.xk_ref, ...), custom_call_target="tpu_custom_call" | custom-call | flops 21474836480 | bytes 94371840 | tf_op jit(solution)/shard_map/norm_back/pallas_call | solution.py:369
  416.0 26.0 %head_grads.3 = f32[160,2560]{1,0:T(8,128)S(1)} custom-call(bf16[4,2,2048,128]{3,2,1,0:T(8,128)(2,1)} %get-tuple-element.56.refs_1_.s_ref, bf16[8192,2560]{1,0:T(8,128)(2,1)} %all-gather.8.cloned.1.call-done.a_ref), custom_call_target="tpu_custom_call" | custom-call | flops 10737418240 | bytes 52428800 | tf_op jit(solution)/shard_map/head_grads/pallas_call | solution.py:326
  447.2 12.4 %token_rows.1 = bf16[16,320,512]{2,1,0:T(8,128)(2,1)} custom-call(bf16[4,2,2048,128]{3,2,1,0:T(8,128)(2,1)} %get-tuple-element.47.s_ref.refs_0_, bf16[4,2,2048,128]{3,2,1,0:T(8,128)(2,1)} %get-tuple-element.56.refs_1_.s_ref), custom_call_target="tpu_custom_call" | custom-call | flops 2621440 | bytes 10485760 | tf_op jit(solution)/shard_map/token_rows/pallas_call | solution.py:296
  459.6 94.8 %all_to_all.15 = bf16[16,320,512]{2,1,0:T(8,128)(2,1)} all-to-all(bf16[16,320,512]{2,1,0:T(8,128)(2,1)} %token_rows.1), channel_id=1, replica_groups=mesh['sp'=16] {'sp'}, dimensions={0} | all-to-all | bytes 10485760 | tf_op jit(solution)/shard_map/all_to_all | solution.py:438
  563.9 5.4 slice_bitcast_fusion
  569.4 105.6 %all-to-all-done.2 = bf16[16,320,512]{2,1,0:T(8,128)(2,1)} async-done(((bf16[16,320,512]{2,1,0:T(8,128)(2,1)}), bf16[16,320,512]{2,1,0:T(8,128)(2,1)}, u32[]{:S(2)}, u32[]{:S(2)}) %all-to-all-start.2) | async-done | bytes 5242912 | tf_op jit(solution)/shard_map/all_to_all | solution.py:440
  683.9 32.1 %fusion.6 = (f32[512]{0:T(512)S(1)}, bf16[512,2560]{1,0:T(8,128)(2,1)S(1)}) fusion(f32[512]{0:T(512)S(1)} %get-tuple-element.81, f32[2560]{0:T(1024)S(1)} %convert_element_type.42, bf16[4,128,2560]{2,1,0:T(8,128)(2,1)S(1)} %copy-done.4, bf16[7680,512]{1,0:T(8,128)(2,1)} %bitcast.79, bf16[2560,7680]{1,0:T(8,128)(2,1)} %param.9), kind=kOutput, calls=%fused_computation.14 | convolution fusion | flops 20141834240 | bytes 52443136 | tf_op jit(solution)/shard_map/dot_general | solution.py:452
  719.6 8.9 %exchange.5 = f32[16,24,128]{2,1,0:T(8,128)} custom-call(f32[24,128]{1,0:T(8,128)} %pad_bitcast_fusion.1.x_ref), custom_call_target="tpu_custom_call" | custom-call | tf_op jit(solution)/shard_map/exchange/pallas_call | solution.py:57
  731.6 5.7 add_convert_fusion
  737.3 11.3 %fusion.7 = bf16[512,2560]{1,0:T(8,128)(2,1)} fusion(bf16[512,2560]{1,0:T(8,128)(2,1)S(1)} %bitcast.77, bf16[2560,512]{1,0:T(8,128)(2,1)S(1)} %bitcast.80, bf16[2560,2560]{1,0:T(8,128)(2,1)} %w_ref.1), kind=kOutput, calls=%fused_computation.15 | convolution fusion | flops 6714818560 | bytes 20971520 | tf_op jit(solution)/shard_map/dot_general | solution.py:452
  748.6 27.5 %place_columns.2.refs_0_ = f32[2560,7680]{1,0:T(8,128)} custom-call(f32[16,160,2560]{2,1,0:T(8,128)} %bitcast.78), custom_call_target="tpu_custom_call" | custom-call | flops 6553600 | bytes 52428800 | tf_op jit(solution)/shard_map/place_columns/pallas_call | solution.py:254
  776.1 28.6 %all-gather.10.cloned.1.call-done = f32[6400,2560]{1,0:T(8,128)} async-done(((f32[400,2560]{1,0:T(8,128)}), f32[6400,2560]{1,0:T(8,128)}) %all-gather.10.cloned.1.call-update) | async-done | bytes 65536016 | tf_op jit(solution)/shard_map/all_gather | solution.py:426
  804.7 9.7 %place_rows.2.refs_0_ = f32[16,2,80,2560]{3,2,1,0:T(8,128)} custom-call(f32[16,400,2560]{2,1,0:T(8,128)} %bitcast.73), custom_call_target="tpu_custom_call" | custom-call | flops 3276800 | bytes 26214400 | tf_op jit(solution)/shard_map/place_rows/pallas_call | solution.py:275
  814.4 54.6 %place_columns.3 = f32[2560,7680]{1,0:T(8,128)} custom-call(f32[16,400,2560]{2,1,0:T(8,128)} %bitcast.74, f32[2560,7680]{1,0:T(8,128)} %place_columns.2.refs_0_), custom_call_target="tpu_custom_call", output_to_operand_aliasing={{}: (1, {})} | custom-call | flops 13107200 | bytes 104857600 | tf_op jit(solution)/shard_map/place_columns/pallas_call | solution.py:254
  (94 shorter events, 81.8 us)
Async XLA Ops:
  7.2 170.2 %all-gather.6.cloned.1.call-start = ((), (), s32[]{:S(2)}) async-start(), calls=%async_computation.3 | async-start | bytes 44564480 | tf_op jit(solution)/shard_map/all_gather | solution.py:404
  13.3 402.7 %all-gather.8.cloned.1.call-start = ((), (), s32[]{:S(2)}) async-start(), calls=%async_computation.4 | async-start | bytes 44564480 | tf_op jit(solution)/shard_map/all_gather | solution.py:421
  35.1 7.0 copy-start.6
  43.6 19.6 %copy-start.14 = (pred[128]{0:T(512)(128)(4,1)S(1)}, pred[128]{0:T(512)(128)(4,1)}, u32[]{:S(2)}) copy-start(pred[128]{0:T(512)(128)(4,1)} %constant.43.clone.1) | copy-start | bytes 388
  60.2 13.8 %copy-start.1 = (bf16[4,128,2560]{2,1,0:T(8,128)(2,1)S(1)}, bf16[4,128,2560]{2,1,0:T(8,128)(2,1)}, u32[]{:S(2)}) copy-start(bf16[4,128,2560]{2,1,0:T(8,128)(2,1)} %param.13) | copy-start | bytes 7864324
  83.5 1.5 copy-start.3
  177.4 54.4 %all-to-all-start = ((bf16[16,160,512]{2,1,0:T(8,128)(2,1)}), bf16[16,160,512]{2,1,0:T(8,128)(2,1)}, u32[]{:S(2)}, u32[]{:S(2)}) async-start(bf16[16,160,512]{2,1,0:T(8,128)(2,1)} %bitcast.72), calls=%async_computation | async-start | bytes 5242880 | tf_op jit(solution)/shard_map/all_to_all | solution.py:412
  180.6 568.0 %all-gather.12.cloned.1.call-start = ((), (), s32[]{:S(2)}) async-start(), calls=%async_computation.6 | async-start | bytes 27852800 | tf_op jit(solution)/shard_map/all_gather | solution.py:426
  322.6 25.8 %copy-start.11 = (f32[4,2,8,2048]{3,2,1,0:T(8,128)S(1)}, f32[4,2,8,2048]{3,2,1,0:T(8,128)}, u32[]{:S(2)}) copy-start(f32[4,2,8,2048]{3,2,1,0:T(8,128)} %get-tuple-element.46) | copy-start | bytes 1572868
  347.1 1.2 copy-start.2
  348.3 456.3 %all-gather.10.cloned.1.call-start = ((), (), s32[]{:S(2)}) async-start(), calls=%async_computation.5 | async-start | bytes 69632000 | tf_op jit(solution)/shard_map/all_gather | solution.py:426
  442.1 2.2 copy-start.9
  446.6 424.6 %all-gather.14.cloned.1.call-start = ((), (), s32[]{:S(2)}) async-start(), calls=%async_computation.7 | async-start | bytes 13926400 | tf_op jit(solution)/shard_map/all_gather | solution.py:426
  554.4 3.7 copy-start.13
  554.4 120.5 %all-to-all-start.2 = ((bf16[16,320,512]{2,1,0:T(8,128)(2,1)}), bf16[16,320,512]{2,1,0:T(8,128)(2,1)}, u32[]{:S(2)}, u32[]{:S(2)}) async-start(bf16[16,320,512]{2,1,0:T(8,128)(2,1)} %get-tuple-element.52), calls=%async_computation.2 | async-start | bytes 10485760 | tf_op jit(solution)/shard_map/all_to_all | solution.py:440
  558.1 5.5 copy-start.12
  675.0 4.2 copy-start.8
  679.2 4.7 copy-start.4
  716.1 2.9 copy-start.7
  731.5 5.7 copy-start.5
  731.6 5.7 copy-start.10
  871.2 4.7 copy-start
Sparse Core Ops, SparseCore 0:
  13.4 163.9 all-gather.5
  179.6 181.5 all-gather.7
  363.4 110.4 all-gather.11
  476.0 328.6 all-gather.9
  806.8 64.3 all-gather.13

commit v4 on v3

--- a/solution.py
+++ b/solution.py
@@ -28,13 +28,6 @@
     return centered * lax.rsqrt(var_val + 1e-5) * weight
 
 
-def row_stats(values):
-    mean = jnp.mean(values, axis=-1, keepdims=True)
-    centered = values - mean
-    var_val = jnp.mean(centered * centered, axis=-1)
-    return mean[..., 0], lax.rsqrt(var_val + 1e-5)
-
-
 def exchange(block, n_dev, scatter=False):
     shape = block.shape[1:] if scatter else block.shape
 
@@ -43,16 +36,22 @@
         src = (lambda dev: x_ref.at[dev]) if scatter else (lambda dev: x_ref)
         own = pltpu.make_async_copy(src(me), o_ref.at[me], loc_sem)
         own.start()
-        copies = []
-        for step in range(1, n_dev):
+
+        def copy(step):
             peer = lax.rem(me + step, n_dev)
-            copies.append(pltpu.make_async_remote_copy(
+            return pltpu.make_async_remote_copy(
                 src_ref=src(peer), dst_ref=o_ref.at[me], send_sem=send_sem.at[step], recv_sem=recv_sem.at[step],
-                device_id=(peer,), device_id_type=MESH))
-            copies[-1].start()
+                device_id=(peer,), device_id_type=MESH)
+
+        @pl.loop(1, n_dev)
+        def _(step):
+            copy(step).start()
+
         own.wait()
-        for copy in copies:
-            copy.wait()
+
+        @pl.loop(1, n_dev)
+        def _(step):
+            copy(step).wait()
 
     return pl.pallas_call(
         kernel,
@@ -99,6 +98,118 @@
         cost_estimate=pl.CostEstimate(flops=2 * n_out * d_in * rows, bytes_accessed=2 * (n_out + rows) * d_in, transcendentals=0),
         name='columns_of',
     )(weight, rows_in)
+
+
+def column_stats(h, w_qkv, blk):
+    rows, d_model = h.shape
+    n_blk = d_model // blk
+
+    def kernel(h_ref, w_ref, o_ref, raw):
+        c = pl.program_id(1)
+        raw[c] = jnp.dot(h_ref[...], w_ref[...], preferred_element_type=F32)
+
+        @pl.when(c == n_blk - 1)
+        def _():
+            mean = sum(jnp.sum(raw[m], axis=1, keepdims=True) for m in range(n_blk)) * (1.0 / d_model)
+            sq = jnp.zeros((rows, 1), F32)
+            for m in range(n_blk):
+                centered = raw[m] - mean
+                sq = sq + jnp.sum(centered * centered, axis=1, keepdims=True)
+            rstd = lax.rsqrt(sq * (1.0 / d_model) + 1e-5)
+            lane = lax.broadcasted_iota(jnp.int32, (rows, LANES), 1)
+            o_ref[0] = jnp.where(lane == 0, mean, rstd)
+
+    return pl.pallas_call(
+        kernel,
+        grid=(2, n_blk),
+        out_shape=jax.ShapeDtypeStruct((2, rows, LANES), F32),
+        in_specs=[pl.BlockSpec((rows, d_model), lambda p, c: (0, 0)), pl.BlockSpec((d_model, blk), lambda p, c: (0, p * n_blk + c))],
+        out_specs=pl.BlockSpec((1, rows, LANES), lambda p, c: (p, 0, 0)),
+        scratch_shapes=[pltpu.VMEM((n_blk, rows, blk), F32)],
+        compiler_params=pltpu.CompilerParams(vmem_limit_bytes=50 * 2 ** 20),
+        cost_estimate=pl.CostEstimate(flops=4 * rows * d_model * d_model, bytes_accessed=4 * d_model * d_model, transcendentals=0),
+        name='column_stats',
+    )(h, w_qkv)
+
+
+def project_out(tok_ov, w_out, x, group):
+    rows, d_model = x.shape
+    n_dev, width = tok_ov.shape[0], tok_ov.shape[1] // 2
+    steps = n_dev // group
+
+    def kernel(o_ref, w_ref, x_ref, y_ref, acc):
+        step = pl.program_id(0)
+
+        @pl.when(step == 0)
+        def _():
+            acc[...] = x_ref[...].astype(F32)
+
+        acc[...] += lax.dot_general(o_ref[...].reshape(group * width, rows), w_ref[...], (((0,), (0,)), ((), ())), preferred_element_type=F32)
+
+        @pl.when(step == steps - 1)
+        def _():
+            y_ref[...] = acc[...].astype(BF16)
+
+    return pl.pallas_call(
+        kernel,
+        grid=(steps,),
+        out_shape=jax.ShapeDtypeStruct((rows, d_model), BF16),
+        in_specs=[pl.BlockSpec((group, width, rows), lambda i: (i, 1, 0)), pl.BlockSpec((group * width, d_model), lambda i: (i, 0)),
+                  pl.BlockSpec((rows, d_model), lambda i: (0, 0))],
+        out_specs=pl.BlockSpec((rows, d_model), lambda i: (0, 0)),
+        scratch_shapes=[pltpu.VMEM((rows, d_model), F32)],
+        compiler_params=pltpu.CompilerParams(vmem_limit_bytes=50 * 2 ** 20),
+        cost_estimate=pl.CostEstimate(flops=2 * rows * d_model * d_model, bytes_accessed=2 * d_model * d_model, transcendentals=0),
+        name='project_out',
+    )(tok_ov, w_out, x)
+
+
+def token_grads(tok_qk, tok_ov, w_qkv, x, ln_w, gy, group, chunk):
+    rows, d_model = x.shape
+    n_dev, width = tok_ov.shape[0], tok_ov.shape[1] // 2
+    steps = n_dev // group
+
+    def kernel(qk_ref, v_ref, w_ref, x_ref, l_ref, y_ref, o_ref, gl_ref, acc):
+        part, step = pl.program_id(0), pl.program_id(1)
+
+        @pl.when((part == 0) & (step == 0))
+        def _():
+            acc[...] = jnp.zeros_like(acc)
+
+        side = jnp.where(part == 2, v_ref[...], qk_ref[...]).reshape(group * width, rows)
+        acc[...] += lax.dot_general(side, w_ref[...], (((0,), (1,)), ((), ())), preferred_element_type=F32)
+
+        @pl.when((part == 2) & (step == steps - 1))
+        def _():
+            gl_ref[...] = jnp.zeros_like(gl_ref)
+
+            @pl.loop(0, rows // chunk)
+            def _(m):
+                at = pl.ds(pl.multiple_of(m * chunk, chunk), chunk)
+                xs = x_ref[at, :].astype(F32)
+                centered = xs - jnp.mean(xs, axis=1, keepdims=True)
+                rstd = lax.rsqrt(jnp.mean(centered * centered, axis=1, keepdims=True) + 1e-5)
+                hat = centered * rstd
+                d_h = acc[at, :].astype(BF16).astype(F32)
+                gl_ref[...] += jnp.sum(d_h * hat, axis=0, keepdims=True)
+                g = d_h * l_ref[...]
+                d_x = rstd * (g - jnp.mean(g, axis=1, keepdims=True) - hat * jnp.mean(g * hat, axis=1, keepdims=True))
+                o_ref[at, :] = (d_x + y_ref[at, :].astype(F32)).astype(BF16)
+
+    whole = pl.BlockSpec((rows, d_model), lambda p, i: (0, 0))
+    line = pl.BlockSpec((1, d_model), lambda p, i: (0, 0))
+    return pl.pallas_call(
+        kernel,
+        grid=(3, steps),
+        out_shape=[jax.ShapeDtypeStruct((rows, d_model), BF16), jax.ShapeDtypeStruct((1, d_model), F32)],
+        in_specs=[pl.BlockSpec((group, width, rows), lambda p, i: (i, jnp.minimum(p, 1), 0)), pl.BlockSpec((group, width, rows), lambda p, i: (i, 0, 0)),
+                  pl.BlockSpec((d_model, group * width), lambda p, i: (0, p * steps + i)), whole, line, whole],
+        out_specs=[whole, line],
+        scratch_shapes=[pltpu.VMEM((rows, d_model), F32)],
+        compiler_params=pltpu.CompilerParams(vmem_limit_bytes=60 * 2 ** 20),
+        cost_estimate=pl.CostEstimate(flops=6 * rows * d_model * d_model, bytes_accessed=6 * d_model * d_model, transcendentals=0),
+        name='token_grads',
+    )(tok_qk, tok_ov, w_qkv, x, ln_w, gy)
 
 
 def token_cols(block, n_batch):
@@ -215,14 +326,16 @@
                 d_s = (p * (d_p - delta)).astype(BF16)
                 dk_acc[blocks[j], :] += dot(d_s, q_b)
                 dq_t = dq_t + dot(kt_ref[:, blocks[j]], d_s)
-            dq_b = (dq_t * scale).T.astype(BF16)
-            dq_ref[0, 0, blocks[i], :] = dq_b
-            norm_terms(0, blocks[i], dq_b, xq_ref, gq_ref)
-
-        for j in range(n_blk):
-            dk_b = (dk_acc[blocks[j], :] * scale).astype(BF16)
-            dk_ref[0, 0, blocks[j], :] = dk_b
-            norm_terms(1, blocks[j], dk_b, xk_ref, gk_ref)
+            dq_ref[0, 0, blocks[i], :] = (dq_t * scale).T.astype(BF16)
+
+        @pl.loop(0, n_blk)
+        def _(j):
+            rows = pl.ds(pl.multiple_of(j * blk, blk), blk)
+            dk_b = (dk_acc[rows, :] * scale).astype(BF16)
+            dk_ref[0, 0, rows, :] = dk_b
+            norm_terms(0, rows, dq_ref[0, 0, rows, :], xq_ref, gq_ref)
+            norm_terms(1, rows, dk_b, xk_ref, gk_ref)
+
         dv_ref[0, 0] = dv_acc[...].astype(BF16)
 
     spec = pl.BlockSpec((1, 1, seq, LANES), lambda b, n: (b, n, 0, 0))
@@ -398,14 +511,13 @@
         def pad_lanes(a):
             return jnp.pad(a, ((0, 0),) * (a.ndim - 1) + ((0, LANES - head_dim),))
 
-        x_flat = x.reshape(rows, d_model).astype(F32)
         gy = grad_y.reshape(rows, d_model)
         h_loc = norm_rows(x.reshape(rows, d_model), ln1_w.astype(F32).reshape(1, d_model), math.gcd(rows, 128))
         h_all = lax.all_gather(h_loc, 'sp', axis=0, tiled=True)
 
-        qk_raw = jnp.dot(h_loc, w_qkv[:, :2 * d_model], preferred_element_type=F32)
-        stats_loc = jnp.stack(row_stats(qk_raw[:, :d_model]) + row_stats(qk_raw[:, d_model:])).reshape(4, n_batch, tok)
-        stats_loc = jnp.pad(stats_loc.transpose(1, 0, 2), ((0, 0), (0, 4), (0, 0))).reshape(8 * n_batch, tok)
+        stats_loc = column_stats(h_loc, w_qkv, d_model // 4)[:, :, :2].reshape(2, n_batch, tok, 2)
+        stats_loc = stats_loc.transpose(1, 0, 3, 2).reshape(n_batch, 4, tok)
+        stats_loc = jnp.pad(stats_loc, ((0, 0), (0, 4), (0, 0))).reshape(8 * n_batch, tok)
         stats = exchange(stats_loc, n_dev)
         d_o = columns_of(w_out, gy, 4 * width).reshape(n_dev, width, rows)
         d_o, h_all = lax.optimization_barrier((d_o, h_all))
@@ -448,18 +560,11 @@
         grad_w_out = place_rows(None, dw_qko, 2 * width, half, 0, 2)
         grad_w_out = place_rows(grad_w_out, dw_last, 0, half, 1, 2).reshape(d_model, d_model)
 
-        def over_rows(cols, weight, w_dim):
-            return lax.dot_general(cols, weight, (((0,), (w_dim,)), ((), ())), preferred_element_type=F32)
-
-        o_cols = tok_ov[:, width:].reshape(d_model, rows)
-        y = (over_rows(o_cols, w_out, 0) + x_flat).astype(BF16)
-        d_cols = jnp.stack([tok_qk[:, :width], tok_qk[:, width:], tok_ov[:, :width]]).reshape(3 * d_model, rows)
-        d_h = over_rows(d_cols, w_qkv, 1).astype(BF16)
-        _, ln1_pull = jax.vjp(layer_norm, x_flat, ln1_w.astype(F32))
-        d_x_norm, grad_ln1 = ln1_pull(d_h.astype(F32))
-        grad_x = (d_x_norm + gy.astype(F32)).astype(BF16)
-
-        small = jnp.concatenate([grad_ln1, grad_q_ln.reshape(-1), grad_k_ln.reshape(-1)])
+        x_rows = x.reshape(rows, d_model)
+        y = project_out(tok_ov, w_out, x_rows, 4)
+        grad_x, grad_ln1 = token_grads(tok_qk, tok_ov, w_qkv, x_rows, ln1_w.astype(F32).reshape(1, d_model), gy, 4, math.gcd(rows, 64))
+
+        small = jnp.concatenate([grad_ln1[0], grad_q_ln.reshape(-1), grad_k_ln.reshape(-1)])
         n_small = small.shape[0]
         pad = -n_small % (8 * LANES)
         small_all = exchange(jnp.pad(small, (0, pad)).reshape(-1, LANES), n_dev).reshape(n_dev, n_small + pad)

time: 899 us -> 888 us (0.988)
  Pallas kernels: 395 us -> 473 us
  matrix products: 65.2 us -> 0 us
  other arithmetic: 37.8 us -> 13.6 us
  waiting for transfers between devices: 238 us -> 258 us
  local copies, waits for them, and re-layouts: 35 us -> 23.6 us
    pallas_call x0 -> x3, Pallas kernels: none -> 80 us  [the longest x1 44 us: token_grads(): pl.pallas_call(kernel, grid=(3, steps), out_shape=[jax.ShapeDtypeStruct((...]
    dot_general x3 -> x0, matrix products: 65.2 us -> none  [the longest x2 43.5 us: over_rows(): lax.dot_general(cols, weight, (((0,), (w_dim,)), ((), ())), preferred_ele...]
    reduce_sum x5 -> x0, other arithmetic: 14.5 us -> none  [the longest x1 4.73 us: row_stats(): mean = jnp.mean(values, axis=-1, keepdims=True)]
    all_to_all x1, waiting for transfers between devices: 106 us -> 117 us  [local_step(): tok_qk = lax.all_to_all(back_qk, 'sp', 0, 0, tiled=True)]
  transfers between devices with their start and end apart: 7 -> 7, of which waited for: 5 -> 5; matrix products, arithmetic and copies ran while one was open for 14% -> 3% of each run, Pallas kernels for 43% -> 52%
where the time goes in v4:
time: 888 us; the launch traced here: 884 us
  Pallas kernels  473 us (53%)
  waiting for transfers between devices  258 us (29%)
  blocking collectives  94.5 us (11%)
  local copies, waits for them, and re-layouts  23.6 us (3%)
  between operations  14 us (2%)
  other arithmetic  13.6 us (2%)
    all_to_all x1, waiting for transfers between devices, local_step(): tok_qk = lax.all_to_all(back_qk, 'sp', 0, 0, tiled=True)  117 us
    all_gather x1, waiting for transfers between devices, local_step(): h_all = lax.all_gather(h_loc, 'sp', axis=0, tiled=True)  98.7 us
    all_to_all x1, blocking collectives, local_step(): lax.all_to_all(token_rows((d_v, o), n_dev, n_batch, tok, head_dim), 'sp',...  94.5 us
    pallas_call x1, Pallas kernels, attention(): pl.pallas_call(kernel, grid=(n_batch, n_h), out_shape=[jax.ShapeDtypeStru...  90.4 us
    pallas_call x2, Pallas kernels, place_columns(): pl.pallas_call(kernel, grid=(parts, n_grp, d_in // mb), out_shape=jax.Sha...  82.3 us
    pallas_call x2, Pallas kernels, head_grads(): pl.pallas_call(kernel, grid=(n_dev,), out_shape=jax.ShapeDtypeStruct((n_h...  51.4 us
    pallas_call x1, Pallas kernels, norm_back(): pl.pallas_call(kernel, grid=(n_dev,), out_shape=[jax.ShapeDtypeStruct((2...  45.2 us
    pallas_call x1, Pallas kernels, token_grads(): pl.pallas_call(kernel, grid=(3, steps), out_shape=[jax.ShapeDtypeStruct((...  44 us
  transfers between devices with their start and end apart: 7, of which 5 were waited for; matrix products, arithmetic and copies ran while one was open for 3% of the time, Pallas kernels for 52%

profile of v4, /device:TPU:1, one launch (start us, length us, event | category | flops | bytes accessed | tf_op | source)
XLA Modules:
  0.0 883.5 jit_solution(3223833797457900914)
XLA Ops:
  8.5 4.8 norm_rows.1.h_ref
  15.1 22.2 %column_stats.1 = f32[2,512,128]{2,1,0:T(8,128)S(1)} custom-call(bf16[512,2560]{1,0:T(8,128)(2,1)S(1)} %copy-done.1, bf16[2560,7680]{1,0:T(8,128)(2,1)} %w_ref.7), custom_call_target="tpu_custom_call" | custom-call | flops 13421772800 | bytes 26214400 | tf_op jit(solution)/shard_map/column_stats/pallas_call | solution.py:122
  38.1 11.4 %exchange.3.st_ref = f32[16,32,128]{2,1,0:T(8,128)} custom-call(f32[32,128]{1,0:T(8,128)} %pad_bitcast_fusion.x_ref), custom_call_target="tpu_custom_call" | custom-call | tf_op jit(solution)/shard_map/exchange/pallas_call | solution.py:56
  65.2 10.7 %columns_of.1 = bf16[2560,512]{1,0:T(8,128)(2,1)} custom-call(bf16[2560,2560]{1,0:T(8,128)(2,1)} %w_ref.6, bf16[512,2560]{1,0:T(8,128)(2,1)S(1)} %bitcast.43), custom_call_target="tpu_custom_call" | custom-call | flops 6710886400 | bytes 15728640 | tf_op jit(solution)/shard_map/columns_of/pallas_call | solution.py:91
  75.9 98.7 %all-gather.6.cloned.1.call-done.h_ref.a_ref = bf16[8192,2560]{1,0:T(8,128)(2,1)} async-done(((bf16[512,2560]{1,0:T(8,128)(2,1)}), bf16[8192,2560]{1,0:T(8,128)(2,1)}) %all-gather.6.cloned.1.call-update) | async-done | bytes 41943056 | tf_op jit(solution)/shard_map/all_gather | solution.py:516
  177.4 41.6 %qkv_heads.1 = (bf16[4,2,2048,128]{3,2,1,0:T(8,128)(2,1)}, bf16[4,2,2048,128]{3,2,1,0:T(8,128)(2,1)}, bf16[4,2,2048,128]{3,2,1,0:T(8,128)(2,1)}, f32[4,2,2048,128]{3,2,1,0:T(8,128)}, f32[4,2,2048,128]{3,2,1,0:T(8,128)}) custom-call(bf16[8192,2560]{1,0:T(8,128)(2,1)} %all-gather.6.cloned.1.call-done.h_ref.a_ref, ...), custom_call_target="tpu_custom_call" | custom-call | flops 32212254720 | bytes 83886080 | tf_op jit(solution)/shard_map/qkv_heads/pallas_call | solution.py:240
  219.0 9.1 %all-to-all-done = bf16[16,160,512]{2,1,0:T(8,128)(2,1)S(1)} async-done(((bf16[16,160,512]{2,1,0:T(8,128)(2,1)}), bf16[16,160,512]{2,1,0:T(8,128)(2,1)S(1)}, u32[]{:S(2)}, u32[]{:S(2)}) %all-to-all-start) | async-done | bytes 2621472 | tf_op jit(solution)/shard_map/all_to_all | solution.py:524
  229.6 90.4 %attention.1 = (bf16[4,2,2048,128]{3,2,1,0:T(8,128)(2,1)}, bf16[4,2,2048,128]{3,2,1,0:T(8,128)(2,1)}, bf16[4,2,2048,128]{3,2,1,0:T(8,128)(2,1)}, bf16[4,2,2048,1...) custom-call(f32[2]{0:T(128)} %dynamic_slice.18.slope_ref, ...), custom_call_target="tpu_custom_call" | custom-call | flops 51539607552 | bytes 41943040 | tf_op jit(solution)/shard_map/attention/pallas_call | solution.py:343
  320.0 25.4 %head_grads.2 = f32[160,2560]{1,0:T(8,128)} custom-call(bf16[4,2,2048,128]{3,2,1,0:T(8,128)(2,1)} %get-tuple-element.49.s_ref.refs_0_, bf16[8192,2560]{1,0:T(8,128)(2,1)} %all-gather.6.cloned.1.call-done.h_ref.a_ref), custom_call_target="tpu_custom_call" | custom-call | flops 10737418240 | bytes 52428800 | tf_op jit(solution)/shard_map/head_grads/pallas_call | solution.py:439
  346.7 10.1 %scatter_rows.1 = f32[16,32,128]{2,1,0:T(8,128)} custom-call(f32[16,32,128]{2,1,0:T(8,128)} %bitcast.54), custom_call_target="tpu_custom_call" | custom-call | tf_op jit(solution)/shard_map/scatter_rows/pallas_call | solution.py:56
  358.3 8.9 %exchange.4.c_ref = f32[16,32,128]{2,1,0:T(8,128)} custom-call(f32[32,128]{1,0:T(8,128)} %broadcast_multiply_fusion.x_ref), custom_call_target="tpu_custom_call" | custom-call | tf_op jit(solution)/shard_map/exchange/pallas_call | solution.py:56
  367.3 45.2 %norm_back.1 = (f32[320,2560]{1,0:T(8,128)}, bf16[16,320,512]{2,1,0:T(8,128)(2,1)}) custom-call(bf16[4,2,2048,128]{3,2,1,0:T(8,128)(2,1)} %get-tuple-element.51.dq_ref, bf16[4,2,2048,128]{3,2,1,0:T(8,128)(2,1)} %get-tuple-element.52.dk_ref, f32[4,2,2048,128]{3,2,1,0:T(8,128)} %get-tuple-element.41.xq_ref, f32[4,2,2048,128]{3,2,1,0:T(8,128)} %get-tuple-element.42.xk_ref, ...), custom_call_target="tpu_custom_call" | custom-call | flops 21474836480 | bytes 94371840 | tf_op jit(solution)/shard_map/norm_back/pallas_call | solution.py:482
  412.5 26.0 %head_grads.3 = f32[160,2560]{1,0:T(8,128)S(1)} custom-call(bf16[4,2,2048,128]{3,2,1,0:T(8,128)(2,1)} %get-tuple-element.60.refs_1_.s_ref, bf16[8192,2560]{1,0:T(8,128)(2,1)} %all-gather.8.cloned.1.call-done.a_ref), custom_call_target="tpu_custom_call" | custom-call | flops 10737418240 | bytes 52428800 | tf_op jit(solution)/shard_map/head_grads/pallas_call | solution.py:439
  443.5 12.4 %token_rows.1 = bf16[16,320,512]{2,1,0:T(8,128)(2,1)} custom-call(bf16[4,2,2048,128]{3,2,1,0:T(8,128)(2,1)} %get-tuple-element.49.s_ref.refs_0_, bf16[4,2,2048,128]{3,2,1,0:T(8,128)(2,1)} %get-tuple-element.60.refs_1_.s_ref), custom_call_target="tpu_custom_call" | custom-call | flops 2621440 | bytes 10485760 | tf_op jit(solution)/shard_map/token_rows/pallas_call | solution.py:409
  455.9 94.5 %all_to_all.15.o_ref.v_ref = bf16[16,320,512]{2,1,0:T(8,128)(2,1)} all-to-all(bf16[16,320,512]{2,1,0:T(8,128)(2,1)} %token_rows.1), channel_id=1, replica_groups=mesh['sp'=16] {'sp'}, dimensions={0} | all-to-all | bytes 10485760 | tf_op jit(solution)/shard_map/all_to_all | solution.py:550
  554.3 116.6 %all-to-all-done.2.qk_ref = bf16[16,320,512]{2,1,0:T(8,128)(2,1)} async-done(((bf16[16,320,512]{2,1,0:T(8,128)(2,1)}), bf16[16,320,512]{2,1,0:T(8,128)(2,1)}, u32[]{:S(2)}, u32[]{:S(2)}) %all-to-all-start.2) | async-done | bytes 5242912 | tf_op jit(solution)/shard_map/all_to_all | solution.py:552
  671.0 44.0 %token_grads.1 = (bf16[512,2560]{1,0:T(8,128)(2,1)}, f32[1,2560]{1,0:T(1,128)}) custom-call(bf16[16,320,512]{2,1,0:T(8,128)(2,1)} %all-to-all-done.2.qk_ref, bf16[16,320,512]{2,1,0:T(8,128)(2,1)} %all_to_all.15.o_ref.v_ref, bf16[2560,7680]{1,0:T(8,128)(2,1)} %w_ref.7, bf16[512,2560]{1,0:T(8,128)(2,1)} %bitcast.45, f32[1,2560]{1,0:T(1,128)} %reshape.100.w_ref.l_ref, ...), custom_call_target="tpu_custom_call" | custom-call | flops 20132659200 | bytes 39321600 | tf_op jit(solution)/shard_map/token_grads/pallas_call | solution.py:201
  716.4 8.8 exchange.5
  728.2 13.7 %project_out.1 = bf16[512,2560]{1,0:T(8,128)(2,1)} custom-call(bf16[16,320,512]{2,1,0:T(8,128)(2,1)} %all_to_all.15.o_ref.v_ref, bf16[2560,2560]{1,0:T(8,128)(2,1)} %w_ref.6, bf16[512,2560]{1,0:T(8,128)(2,1)S(1)} %bitcast.46), custom_call_target="tpu_custom_call" | custom-call | flops 6710886400 | bytes 13107200 | tf_op jit(solution)/shard_map/project_out/pallas_call | solution.py:153
  742.0 27.6 %place_columns.2.refs_0_ = f32[2560,7680]{1,0:T(8,128)} custom-call(f32[16,160,2560]{2,1,0:T(8,128)} %bitcast.51), custom_call_target="tpu_custom_call" | custom-call | flops 6553600 | bytes 52428800 | tf_op jit(solution)/shard_map/place_columns/pallas_call | solution.py:367
  769.6 31.1 %all-gather.10.cloned.1.call-done = f32[6400,2560]{1,0:T(8,128)} async-done(((f32[400,2560]{1,0:T(8,128)}), f32[6400,2560]{1,0:T(8,128)}) %all-gather.10.cloned.1.call-update) | async-done | bytes 65536016 | tf_op jit(solution)/shard_map/all_gather | solution.py:538
  800.7 9.7 %place_rows.2.refs_0_ = f32[16,2,80,2560]{3,2,1,0:T(8,128)} custom-call(f32[16,400,2560]{2,1,0:T(8,128)} %bitcast.48), custom_call_target="tpu_custom_call" | custom-call | flops 3276800 | bytes 26214400 | tf_op jit(solution)/shard_map/place_rows/pallas_call | solution.py:388
  810.4 54.6 %place_columns.3 = f32[2560,7680]{1,0:T(8,128)} custom-call(f32[16,400,2560]{2,1,0:T(8,128)} %bitcast.49, f32[2560,7680]{1,0:T(8,128)} %place_columns.2.refs_0_), custom_call_target="tpu_custom_call", output_to_operand_aliasing={{}: (1, {})} | custom-call | flops 13107200 | bytes 104857600 | tf_op jit(solution)/shard_map/place_columns/pallas_call | solution.py:367
  872.0 5.1 place_rows.3
  (67 shorter events, 46.9 us)
Async XLA Ops:
  7.2 167.4 %all-gather.6.cloned.1.call-start = ((), (), s32[]{:S(2)}) async-start(), calls=%async_computation.3 | async-start | bytes 44564480 | tf_op jit(solution)/shard_map/all_gather | solution.py:516
  13.3 399.2 %all-gather.8.cloned.1.call-start = ((), (), s32[]{:S(2)}) async-start(), calls=%async_computation.4 | async-start | bytes 44564480 | tf_op jit(solution)/shard_map/all_gather | solution.py:533
  13.4 1.7 copy-start.1
  37.3 17.0 %copy-start.8 = (pred[128]{0:T(512)(128)(4,1)S(1)}, pred[128]{0:T(512)(128)(4,1)}, u32[]{:S(2)}) copy-start(pred[128]{0:T(512)(128)(4,1)} %constant.30.clone.1) | copy-start | bytes 388
  54.3 10.9 %copy-start.2 = (bf16[4,128,2560]{2,1,0:T(8,128)(2,1)S(1)}, bf16[4,128,2560]{2,1,0:T(8,128)(2,1)}, u32[]{:S(2)}) copy-start(bf16[4,128,2560]{2,1,0:T(8,128)(2,1)} %param.13) | copy-start | bytes 7864324
  174.6 53.6 %all-to-all-start = ((bf16[16,160,512]{2,1,0:T(8,128)(2,1)}), bf16[16,160,512]{2,1,0:T(8,128)(2,1)S(1)}, u32[]{:S(2)}, u32[]{:S(2)}) async-start(bf16[16,160,512]{2,1,0:T(8,128)(2,1)} %bitcast.1), calls=%async_computation | async-start | bytes 5242880 | tf_op jit(solution)/shard_map/all_to_all | solution.py:524
  177.2 564.8 %all-gather.12.cloned.1.call-start = ((), (), s32[]{:S(2)}) async-start(), calls=%async_computation.6 | async-start | bytes 27852800 | tf_op jit(solution)/shard_map/all_gather | solution.py:538
  228.2 1.5 copy-start.5
  320.0 25.7 %copy-start.6 = (f32[4,2,8,2048]{3,2,1,0:T(8,128)S(1)}, f32[4,2,8,2048]{3,2,1,0:T(8,128)}, u32[]{:S(2)}) copy-start(f32[4,2,8,2048]{3,2,1,0:T(8,128)} %get-tuple-element.48) | copy-start | bytes 1572868
  345.5 455.2 %all-gather.10.cloned.1.call-start = ((), (), s32[]{:S(2)}) async-start(), calls=%async_computation.5 | async-start | bytes 69632000 | tf_op jit(solution)/shard_map/all_gather | solution.py:538
  438.5 2.2 copy-start.4
  442.9 424.3 %all-gather.14.cloned.1.call-start = ((), (), s32[]{:S(2)}) async-start(), calls=%async_computation.7 | async-start | bytes 13926400 | tf_op jit(solution)/shard_map/all_gather | solution.py:538
  550.4 3.7 copy-start.7
  550.4 120.6 %all-to-all-start.2 = ((bf16[16,320,512]{2,1,0:T(8,128)(2,1)}), bf16[16,320,512]{2,1,0:T(8,128)(2,1)}, u32[]{:S(2)}, u32[]{:S(2)}) async-start(bf16[16,320,512]{2,1,0:T(8,128)(2,1)} %get-tuple-element.54), calls=%async_computation.2 | async-start | bytes 10485760 | tf_op jit(solution)/shard_map/all_to_all | solution.py:552
  554.3 173.9 %copy-start.3 = (bf16[4,128,2560]{2,1,0:T(8,128)(2,1)S(1)}, bf16[4,128,2560]{2,1,0:T(8,128)(2,1)}, u32[]{:S(2)}) copy-start(bf16[4,128,2560]{2,1,0:T(8,128)(2,1)} %param.7) | copy-start | bytes 7864324
  867.2 4.7 copy-start
Sparse Core Ops, SparseCore 0:
  13.4 161.0 all-gather.5
  176.8 180.3 all-gather.7
  359.4 109.8 all-gather.11
  471.4 329.2 all-gather.9
  802.8 64.3 all-gather.13

commit v5 on v4

--- a/solution.py
+++ b/solution.py
@@ -273,7 +273,7 @@
             gain = g_ref[0]
             prod = d_b.astype(F32) * x_ref[0, 0, rows, :]
             gl_ref[0, 0, part:part + 1, :] += jnp.sum(prod, axis=0, keepdims=True)
-            prod = prod * gain
+            prod = prod * gain * 0.0625
             pieces = [d_b]
             for _ in range(3):
                 pieces.append(prod.astype(BF16))
@@ -283,7 +283,8 @@
             other = jnp.where(row == 1, 1.0, 0.0).astype(BF16)
             lhs = jnp.concatenate([first, other, other, other], axis=1)
             both = lax.dot_general(lhs, jnp.concatenate(pieces, axis=1), (((1,), (1,)), ((), ())), preferred_element_type=F32)
-            sum_ref[0, 0, 2 * part:2 * part + 2, rows] = both[:2]
+            sum_ref[0, 0, 2 * part:2 * part + 1, rows] = both[:1]
+            sum_ref[0, 0, 2 * part + 1:2 * part + 2, rows] = both[1:2] * 16.0
 
         key_iota = lax.broadcasted_iota(jnp.int32, (blk, LANES), 0)[:, :1]
         blocks = [pl.ds(j * blk, blk) for j in range(n_blk)]

time: 888 us -> 888 us (level)
  no operation moved by 1% of the time
where the time goes in v5:
time: 888 us; the launch traced here: 883 us
  Pallas kernels  473 us (53%)
  waiting for transfers between devices  258 us (29%)
  blocking collectives  94.4 us (11%)
  local copies, waits for them, and re-layouts  23.6 us (3%)
  between operations  14 us (2%)
  other arithmetic  13.6 us (2%)
    all_to_all x1, waiting for transfers between devices, local_step(): tok_qk = lax.all_to_all(back_qk, 'sp', 0, 0, tiled=True)  117 us
    all_gather x1, waiting for transfers between devices, local_step(): h_all = lax.all_gather(h_loc, 'sp', axis=0, tiled=True)  98.7 us
    all_to_all x1, blocking collectives, local_step(): lax.all_to_all(token_rows((d_v, o), n_dev, n_batch, tok, head_dim), 'sp',...  94.4 us
    pallas_call x1, Pallas kernels, attention(): pl.pallas_call(kernel, grid=(n_batch, n_h), out_shape=[jax.ShapeDtypeStru...  90.6 us
    pallas_call x2, Pallas kernels, place_columns(): pl.pallas_call(kernel, grid=(parts, n_grp, d_in // mb), out_shape=jax.Sha...  82.2 us
    pallas_call x2, Pallas kernels, head_grads(): pl.pallas_call(kernel, grid=(n_dev,), out_shape=jax.ShapeDtypeStruct((n_h...  51.3 us
    pallas_call x1, Pallas kernels, norm_back(): pl.pallas_call(kernel, grid=(n_dev,), out_shape=[jax.ShapeDtypeStruct((2...  44.9 us
    pallas_call x1, Pallas kernels, token_grads(): pl.pallas_call(kernel, grid=(3, steps), out_shape=[jax.ShapeDtypeStruct((...  44 us
  transfers between devices with their start and end apart: 7, of which 5 were waited for; matrix products, arithmetic and copies ran while one was open for 3% of the time, Pallas kernels for 52%

profile of v5, /device:TPU:1, one launch (start us, length us, event | category | flops | bytes accessed | tf_op | source)
XLA Modules:
  0.0 883.4 jit_solution(7759207118988715343)
XLA Ops:
  8.5 4.8 norm_rows.1.h_ref
  15.1 22.2 %column_stats.1 = f32[2,512,128]{2,1,0:T(8,128)S(1)} custom-call(bf16[512,2560]{1,0:T(8,128)(2,1)S(1)} %copy-done.1, bf16[2560,7680]{1,0:T(8,128)(2,1)} %w_ref.7), custom_call_target="tpu_custom_call" | custom-call | flops 13421772800 | bytes 26214400 | tf_op jit(solution)/shard_map/column_stats/pallas_call | solution.py:122
  38.1 11.4 %exchange.3.st_ref = f32[16,32,128]{2,1,0:T(8,128)} custom-call(f32[32,128]{1,0:T(8,128)} %pad_bitcast_fusion.x_ref), custom_call_target="tpu_custom_call" | custom-call | tf_op jit(solution)/shard_map/exchange/pallas_call | solution.py:56
  65.2 10.7 %columns_of.1 = bf16[2560,512]{1,0:T(8,128)(2,1)} custom-call(bf16[2560,2560]{1,0:T(8,128)(2,1)} %w_ref.6, bf16[512,2560]{1,0:T(8,128)(2,1)S(1)} %bitcast.43), custom_call_target="tpu_custom_call" | custom-call | flops 6710886400 | bytes 15728640 | tf_op jit(solution)/shard_map/columns_of/pallas_call | solution.py:91
  75.9 98.7 %all-gather.6.cloned.1.call-done.h_ref.a_ref = bf16[8192,2560]{1,0:T(8,128)(2,1)} async-done(((bf16[512,2560]{1,0:T(8,128)(2,1)}), bf16[8192,2560]{1,0:T(8,128)(2,1)}) %all-gather.6.cloned.1.call-update) | async-done | bytes 41943056 | tf_op jit(solution)/shard_map/all_gather | solution.py:517
  177.4 41.6 %qkv_heads.1 = (bf16[4,2,2048,128]{3,2,1,0:T(8,128)(2,1)}, bf16[4,2,2048,128]{3,2,1,0:T(8,128)(2,1)}, bf16[4,2,2048,128]{3,2,1,0:T(8,128)(2,1)}, f32[4,2,2048,128]{3,2,1,0:T(8,128)}, f32[4,2,2048,128]{3,2,1,0:T(8,128)}) custom-call(bf16[8192,2560]{1,0:T(8,128)(2,1)} %all-gather.6.cloned.1.call-done.h_ref.a_ref, ...), custom_call_target="tpu_custom_call" | custom-call | flops 32212254720 | bytes 83886080 | tf_op jit(solution)/shard_map/qkv_heads/pallas_call | solution.py:240
  219.0 9.1 %all-to-all-done = bf16[16,160,512]{2,1,0:T(8,128)(2,1)S(1)} async-done(((bf16[16,160,512]{2,1,0:T(8,128)(2,1)}), bf16[16,160,512]{2,1,0:T(8,128)(2,1)S(1)}, u32[]{:S(2)}, u32[]{:S(2)}) %all-to-all-start) | async-done | bytes 2621472 | tf_op jit(solution)/shard_map/all_to_all | solution.py:525
  229.6 90.6 %attention.1 = (bf16[4,2,2048,128]{3,2,1,0:T(8,128)(2,1)}, bf16[4,2,2048,128]{3,2,1,0:T(8,128)(2,1)}, bf16[4,2,2048,128]{3,2,1,0:T(8,128)(2,1)}, bf16[4,2,2048,1...) custom-call(f32[2]{0:T(128)} %dynamic_slice.18.slope_ref, ...), custom_call_target="tpu_custom_call" | custom-call | flops 51539607552 | bytes 41943040 | tf_op jit(solution)/shard_map/attention/pallas_call | solution.py:344
  320.2 25.4 %head_grads.2 = f32[160,2560]{1,0:T(8,128)} custom-call(bf16[4,2,2048,128]{3,2,1,0:T(8,128)(2,1)} %get-tuple-element.49.s_ref.refs_0_, bf16[8192,2560]{1,0:T(8,128)(2,1)} %all-gather.6.cloned.1.call-done.h_ref.a_ref), custom_call_target="tpu_custom_call" | custom-call | flops 10737418240 | bytes 52428800 | tf_op jit(solution)/shard_map/head_grads/pallas_call | solution.py:440
  346.8 10.3 %scatter_rows.1 = f32[16,32,128]{2,1,0:T(8,128)} custom-call(f32[16,32,128]{2,1,0:T(8,128)} %bitcast.54), custom_call_target="tpu_custom_call" | custom-call | tf_op jit(solution)/shard_map/scatter_rows/pallas_call | solution.py:56
  358.7 8.9 %exchange.4.c_ref = f32[16,32,128]{2,1,0:T(8,128)} custom-call(f32[32,128]{1,0:T(8,128)} %broadcast_multiply_fusion.x_ref), custom_call_target="tpu_custom_call" | custom-call | tf_op jit(solution)/shard_map/exchange/pallas_call | solution.py:56
  367.7 44.9 %norm_back.1 = (f32[320,2560]{1,0:T(8,128)}, bf16[16,320,512]{2,1,0:T(8,128)(2,1)}) custom-call(bf16[4,2,2048,128]{3,2,1,0:T(8,128)(2,1)} %get-tuple-element.51.dq_ref, bf16[4,2,2048,128]{3,2,1,0:T(8,128)(2,1)} %get-tuple-element.52.dk_ref, f32[4,2,2048,128]{3,2,1,0:T(8,128)} %get-tuple-element.41.xq_ref, f32[4,2,2048,128]{3,2,1,0:T(8,128)} %get-tuple-element.42.xk_ref, ...), custom_call_target="tpu_custom_call" | custom-call | flops 21474836480 | bytes 94371840 | tf_op jit(solution)/shard_map/norm_back/pallas_call | solution.py:483
  412.6 25.9 %head_grads.3 = f32[160,2560]{1,0:T(8,128)S(1)} custom-call(bf16[4,2,2048,128]{3,2,1,0:T(8,128)(2,1)} %get-tuple-element.60.refs_1_.s_ref, bf16[8192,2560]{1,0:T(8,128)(2,1)} %all-gather.8.cloned.1.call-done.a_ref), custom_call_target="tpu_custom_call" | custom-call | flops 10737418240 | bytes 52428800 | tf_op jit(solution)/shard_map/head_grads/pallas_call | solution.py:440
  443.6 12.4 %token_rows.1 = bf16[16,320,512]{2,1,0:T(8,128)(2,1)} custom-call(bf16[4,2,2048,128]{3,2,1,0:T(8,128)(2,1)} %get-tuple-element.49.s_ref.refs_0_, bf16[4,2,2048,128]{3,2,1,0:T(8,128)(2,1)} %get-tuple-element.60.refs_1_.s_ref), custom_call_target="tpu_custom_call" | custom-call | flops 2621440 | bytes 10485760 | tf_op jit(solution)/shard_map/token_rows/pallas_call | solution.py:410
  456.0 94.4 %all_to_all.15.o_ref.v_ref = bf16[16,320,512]{2,1,0:T(8,128)(2,1)} all-to-all(bf16[16,320,512]{2,1,0:T(8,128)(2,1)} %token_rows.1), channel_id=1, replica_groups=mesh['sp'=16] {'sp'}, dimensions={0} | all-to-all | bytes 10485760 | tf_op jit(solution)/shard_map/all_to_all | solution.py:551
  554.3 116.6 %all-to-all-done.2.qk_ref = bf16[16,320,512]{2,1,0:T(8,128)(2,1)} async-done(((bf16[16,320,512]{2,1,0:T(8,128)(2,1)}), bf16[16,320,512]{2,1,0:T(8,128)(2,1)}, u32[]{:S(2)}, u32[]{:S(2)}) %all-to-all-start.2) | async-done | bytes 5242912 | tf_op jit(solution)/shard_map/all_to_all | solution.py:553
  670.9 44.0 %token_grads.1 = (bf16[512,2560]{1,0:T(8,128)(2,1)}, f32[1,2560]{1,0:T(1,128)}) custom-call(bf16[16,320,512]{2,1,0:T(8,128)(2,1)} %all-to-all-done.2.qk_ref, bf16[16,320,512]{2,1,0:T(8,128)(2,1)} %all_to_all.15.o_ref.v_ref, bf16[2560,7680]{1,0:T(8,128)(2,1)} %w_ref.7, bf16[512,2560]{1,0:T(8,128)(2,1)} %bitcast.45, f32[1,2560]{1,0:T(1,128)} %reshape.100.w_ref.l_ref, ...), custom_call_target="tpu_custom_call" | custom-call | flops 20132659200 | bytes 39321600 | tf_op jit(solution)/shard_map/token_grads/pallas_call | solution.py:201
  716.4 8.7 exchange.5
  728.1 13.8 %project_out.1 = bf16[512,2560]{1,0:T(8,128)(2,1)} custom-call(bf16[16,320,512]{2,1,0:T(8,128)(2,1)} %all_to_all.15.o_ref.v_ref, bf16[2560,2560]{1,0:T(8,128)(2,1)} %w_ref.6, bf16[512,2560]{1,0:T(8,128)(2,1)S(1)} %bitcast.46), custom_call_target="tpu_custom_call" | custom-call | flops 6710886400 | bytes 13107200 | tf_op jit(solution)/shard_map/project_out/pallas_call | solution.py:153
  741.9 27.5 %place_columns.2.refs_0_ = f32[2560,7680]{1,0:T(8,128)} custom-call(f32[16,160,2560]{2,1,0:T(8,128)} %bitcast.51), custom_call_target="tpu_custom_call" | custom-call | flops 6553600 | bytes 52428800 | tf_op jit(solution)/shard_map/place_columns/pallas_call | solution.py:368
  769.5 31.1 %all-gather.10.cloned.1.call-done = f32[6400,2560]{1,0:T(8,128)} async-done(((f32[400,2560]{1,0:T(8,128)}), f32[6400,2560]{1,0:T(8,128)}) %all-gather.10.cloned.1.call-update) | async-done | bytes 65536016 | tf_op jit(solution)/shard_map/all_gather | solution.py:539
  800.6 9.7 %place_rows.2.refs_0_ = f32[16,2,80,2560]{3,2,1,0:T(8,128)} custom-call(f32[16,400,2560]{2,1,0:T(8,128)} %bitcast.48), custom_call_target="tpu_custom_call" | custom-call | flops 3276800 | bytes 26214400 | tf_op jit(solution)/shard_map/place_rows/pallas_call | solution.py:389
  810.3 54.6 %place_columns.3 = f32[2560,7680]{1,0:T(8,128)} custom-call(f32[16,400,2560]{2,1,0:T(8,128)} %bitcast.49, f32[2560,7680]{1,0:T(8,128)} %place_columns.2.refs_0_), custom_call_target="tpu_custom_call", output_to_operand_aliasing={{}: (1, {})} | custom-call | flops 13107200 | bytes 104857600 | tf_op jit(solution)/shard_map/place_columns/pallas_call | solution.py:368
  871.8 5.1 place_rows.3
  (67 shorter events, 47.0 us)
Async XLA Ops:
  7.2 167.4 %all-gather.6.cloned.1.call-start = ((), (), s32[]{:S(2)}) async-start(), calls=%async_computation.3 | async-start | bytes 44564480 | tf_op jit(solution)/shard_map/all_gather | solution.py:517
  13.3 399.2 %all-gather.8.cloned.1.call-start = ((), (), s32[]{:S(2)}) async-start(), calls=%async_computation.4 | async-start | bytes 44564480 | tf_op jit(solution)/shard_map/all_gather | solution.py:534
  13.4 1.7 copy-start.1
  37.3 17.0 %copy-start.8 = (pred[128]{0:T(512)(128)(4,1)S(1)}, pred[128]{0:T(512)(128)(4,1)}, u32[]{:S(2)}) copy-start(pred[128]{0:T(512)(128)(4,1)} %constant.30.clone.1) | copy-start | bytes 388
  54.3 10.9 %copy-start.2 = (bf16[4,128,2560]{2,1,0:T(8,128)(2,1)S(1)}, bf16[4,128,2560]{2,1,0:T(8,128)(2,1)}, u32[]{:S(2)}) copy-start(bf16[4,128,2560]{2,1,0:T(8,128)(2,1)} %param.13) | copy-start | bytes 7864324
  174.6 53.6 %all-to-all-start = ((bf16[16,160,512]{2,1,0:T(8,128)(2,1)}), bf16[16,160,512]{2,1,0:T(8,128)(2,1)S(1)}, u32[]{:S(2)}, u32[]{:S(2)}) async-start(bf16[16,160,512]{2,1,0:T(8,128)(2,1)} %bitcast.1), calls=%async_computation | async-start | bytes 5242880 | tf_op jit(solution)/shard_map/all_to_all | solution.py:525
  177.2 564.7 %all-gather.12.cloned.1.call-start = ((), (), s32[]{:S(2)}) async-start(), calls=%async_computation.6 | async-start | bytes 27852800 | tf_op jit(solution)/shard_map/all_gather | solution.py:539
  228.2 1.5 copy-start.5
  320.2 25.7 %copy-start.6 = (f32[4,2,8,2048]{3,2,1,0:T(8,128)S(1)}, f32[4,2,8,2048]{3,2,1,0:T(8,128)}, u32[]{:S(2)}) copy-start(f32[4,2,8,2048]{3,2,1,0:T(8,128)} %get-tuple-element.48) | copy-start | bytes 1572868
  345.7 454.9 %all-gather.10.cloned.1.call-start = ((), (), s32[]{:S(2)}) async-start(), calls=%async_computation.5 | async-start | bytes 69632000 | tf_op jit(solution)/shard_map/all_gather | solution.py:539
  438.5 2.2 copy-start.4
  443.0 424.1 %all-gather.14.cloned.1.call-start = ((), (), s32[]{:S(2)}) async-start(), calls=%async_computation.7 | async-start | bytes 13926400 | tf_op jit(solution)/shard_map/all_gather | solution.py:539
  550.3 3.8 copy-start.7
  550.3 120.6 %all-to-all-start.2 = ((bf16[16,320,512]{2,1,0:T(8,128)(2,1)}), bf16[16,320,512]{2,1,0:T(8,128)(2,1)}, u32[]{:S(2)}, u32[]{:S(2)}) async-start(bf16[16,320,512]{2,1,0:T(8,128)(2,1)} %get-tuple-element.54), calls=%async_computation.2 | async-start | bytes 10485760 | tf_op jit(solution)/shard_map/all_to_all | solution.py:553
  554.3 173.8 %copy-start.3 = (bf16[4,128,2560]{2,1,0:T(8,128)(2,1)S(1)}, bf16[4,128,2560]{2,1,0:T(8,128)(2,1)}, u32[]{:S(2)}) copy-start(bf16[4,128,2560]{2,1,0:T(8,128)(2,1)} %param.7) | copy-start | bytes 7864324
  867.1 4.7 copy-start
Sparse Core Ops, SparseCore 0:
  13.4 161.0 all-gather.5
  176.8 180.3 all-gather.7
  359.4 109.3 all-gather.11
  470.9 329.6 all-gather.9
  802.7 64.3 all-gather.13
